TPU v7x, 32 devices: a whole 2x2x4 slice. The times are simulated.
32 devices in a mesh: rows: 8 (over y, x, core), cols: 4 (over z).
Axes of the slice: x: 2, y: 2, z: 4, core: 2. Of those that a mesh axis runs over, the one named last changes fastest.
Arguments:
- fmap1: bfloat16 [2, 256, 256, 256], P(None, 'rows', 'cols'), may hold values from -6 to 6
- fmap2: bfloat16 [2, 256, 256, 256], P(None, 'rows', 'cols'), may hold values from -6 to 6
- target_owner: int32 [2, 2048, 1], P(None, ('rows', 'cols')), may hold values from 0 to 31; in each aligned block of 64 rows (0 to 63, 64 to 127, ..., all dimensions but the last counted through in order) at most 4 rows name the same one
- target_tile: int32 [2, 2048], P(None, ('rows', 'cols')), may hold values from 0 to 31
Outputs:
- corr: float32 [2, 81, 131072], P(None, None, ('rows', 'cols'))
Inputs may be any that keep to these rules, and one draw needn't show every extreme that they name: `target_owner`: at each level, the 64 query blocks of one region (aligned blocks of rows) name any one owner at most 4 times, a bound that some block reaches. `target_tile`: tile of the owner's region in the query block's frame, numbered row-major; level l uses it modulo that level's tile count.
All inputs are finite; a program needn't handle non-finite values.
Results may differ from a plain program's by a relative error of at most 0.0013.
Values may be sent and summed in bfloat16 or wider, within the bound.
A program may use at most 128 MiB of HBM per device.

v0:
```python
import jax
import jax.numpy as jnp
from jax import lax
from jax.sharding import PartitionSpec as P

RADIUS = 4
LEVELS = 2


def padded_2(block, sides, width):
    for axis, dim in sides:
        count = lax.axis_size(axis)
        forward = [(i, i + 1) for i in range(count - 1)]
        backward = [(target, source) for source, target in forward]
        low = lax.ppermute(
            lax.slice_in_dim(block, block.shape[dim] - width, None, axis=dim), axis, forward
        )
        high = lax.ppermute(lax.slice_in_dim(block, 0, width, axis=dim), axis, backward)
        block = jnp.concatenate([low, block, high], axis=dim)
    return block


def window_index():
    tile_side = 2 * RADIUS
    span_side = 4 * RADIUS
    window_side = 2 * RADIUS + 1
    query_ids = jnp.arange(tile_side * tile_side, dtype=jnp.int32)
    offset_ids = jnp.arange(window_side * window_side, dtype=jnp.int32)
    row_part = query_ids[:, None] // tile_side + offset_ids[None, :] // window_side
    col_part = query_ids[:, None] % tile_side + offset_ids[None, :] % window_side
    return row_part * span_side + col_part


def pool_level(level_map):
    frame_count, rows_in, cols_in, channels = level_map.shape
    pooled = level_map.astype(jnp.float32).reshape(
        frame_count, rows_in // 2, 2, cols_in // 2, 2, channels
    )
    return jnp.mean(pooled, axis=(2, 4)).astype(jnp.bfloat16)


def body(fmap1, fmap2, target_owner, target_tile):
    tile_side = 2 * RADIUS
    span_side = 4 * RADIUS
    window_side = 2 * RADIUS + 1
    row_width = tile_side * tile_side * window_side * window_side
    group_size = 32
    frame_count, band_rows, band_cols, channels = fmap1.shape
    row_count = lax.axis_size("rows")
    col_count = lax.axis_size("cols")
    device_count = row_count * col_count
    tiles_across = band_cols // tile_side
    per_frame = band_rows // tile_side * tiles_across
    block_count = frame_count * per_frame
    owner_slots = max(2, (2 * block_count + device_count - 1) // device_count)
    slot_count = LEVELS * owner_slots
    levels = [fmap2]
    level = 1
    levels.append(pool_level(levels[-1]))
    padded = [padded_2(level_map, (("rows", 1), ("cols", 2)), RADIUS) for level_map in levels]
    queries = fmap1.reshape(
        frame_count, band_rows // tile_side, tile_side, tiles_across, tile_side, channels
    )
    queries = queries.transpose(0, 1, 3, 2, 4, 5).reshape(
        block_count, tile_side * tile_side, channels
    )
    owner_ids = target_owner[:, :, 0]
    peer_ids = jnp.arange(device_count, dtype=jnp.int32)
    owner_hits = (owner_ids[:, :, None] == peer_ids[None, None, :]).astype(jnp.int32)
    slot_rank = jnp.sum(owner_hits * (jnp.cumsum(owner_hits, axis=1) - 1), axis=2)
    slot_ids = (jnp.arange(LEVELS, dtype=jnp.int32)[:, None] * owner_slots + slot_rank).reshape(-1)
    owner_flat = owner_ids.reshape(-1)
    frame_ids = jnp.arange(block_count, dtype=jnp.int32) // per_frame
    label_rows = []
    for level in range(LEVELS):
        tile_count = (band_rows >> level) // tile_side * ((band_cols >> level) // tile_side)
        label_rows.append(
            (level * frame_count + frame_ids) * per_frame + target_tile[level] % tile_count
        )
    labels_sent = (
        jnp.full((device_count, slot_count), -1, jnp.int32)
        .at[owner_flat, slot_ids]
        .set(jnp.stack(label_rows).reshape(-1))
    )
    query_copies = jnp.broadcast_to(queries[None], (LEVELS,) + queries.shape).reshape(
        LEVELS * block_count, tile_side * tile_side, channels
    )
    queries_sent = (
        jnp.zeros((device_count, slot_count, tile_side * tile_side, channels), jnp.bfloat16)
        .at[owner_flat, slot_ids]
        .set(query_copies)
    )
    window_ids = window_index()

    def correlate(query_rows, label):
        is_live = label >= 0
        label_id = jnp.maximum(label, 0)
        level_ids = label_id // (frame_count * per_frame)
        frame_id = label_id // per_frame % frame_count
        tile_ids = label_id % per_frame
        target_cells = None
        for level in range(LEVELS):
            level_across = (band_cols >> level) // tile_side
            candidate = lax.dynamic_slice(
                padded[level],
                (
                    frame_id,
                    tile_ids // level_across * tile_side,
                    tile_ids % level_across * tile_side,
                    0 * frame_id,
                ),
                (1, span_side, span_side, channels),
            )
            if target_cells is None:
                target_cells = candidate
            else:
                target_cells = jnp.where(level_ids == level, candidate, target_cells)
        scores = jnp.einsum(
            "qc,pc->qp",
            query_rows,
            target_cells.reshape(span_side * span_side, channels),
            preferred_element_type=jnp.float32,
        ) * channels ** (-0.5)
        correlation = jnp.take_along_axis(scores, window_ids, axis=1)
        return jnp.where(is_live, correlation, 0.0).reshape(-1)

    def group_rows(pieces):
        return jax.vmap(correlate)(pieces[0], pieces[1])

    query_part = lax.all_to_all(
        queries_sent, ("rows", "cols"), split_axis=0, concat_axis=0, tiled=True
    )
    label_part = lax.all_to_all(
        labels_sent, ("rows", "cols"), split_axis=0, concat_axis=0, tiled=True
    )
    lead_shape = query_part.shape[:2]
    query_slots = query_part.reshape((-1,) + query_part.shape[2:])
    labels = label_part.reshape(-1)
    slot_total = labels.shape[0]
    round_count = -(-slot_total // group_size)
    padded_total = round_count * group_size
    grouped = lax.map(
        group_rows,
        (
            query_slots.reshape(round_count, group_size, tile_side * tile_side, channels),
            labels.reshape(round_count, group_size),
        ),
    )
    result_rows = grouped.reshape(padded_total, row_width)
    replies = result_rows.reshape(lead_shape + (row_width,))
    returned = lax.all_to_all(
        replies.reshape(device_count, slot_count * row_width),
        ("rows", "cols"),
        split_axis=0,
        concat_axis=0,
        tiled=True,
    )
    reply_table = returned.reshape(device_count, slot_count, row_width)
    own_rows = reply_table[owner_flat, slot_ids].reshape(
        LEVELS, block_count, tile_side * tile_side, window_side * window_side
    )
    return own_rows.transpose(0, 3, 1, 2).reshape(
        LEVELS, window_side * window_side, block_count * tile_side * tile_side
    )


def solution(mesh):
    in_specs = (
        P(None, "rows", "cols", None),
        P(None, "rows", "cols", None),
        P(None, ("rows", "cols"), None),
        P(None, ("rows", "cols")),
    )
    out_specs = P(None, None, ("rows", "cols"))
    return jax.shard_map(body, mesh=mesh, in_specs=in_specs, out_specs=out_specs, check_vma=False)
```

profile of v0, /device:TPU:0, one launch (start us, length us, event | category | flops | bytes accessed | tf_op | source)
XLA Modules:
  0.0 1319.6 jit_solution(13921206460114118143)
XLA Ops:
  28.3 20.7 %scatter_fusion.1 = bf16[32,8,64,256]{3,2,1,0:T(8,128)(2,1)} fusion(bf16[32,8,64,256]{3,2,1,0:T(8,128)(2,1)} %broadcast_in_dim.40, s32[128]{0:T(128)S(1)} %get-tuple-element.226, bf16[128,64,256]{2,1,0:T(8,128)(2,1)} %bitcast.91), kind=kCustom, calls=%fused_computation.5 | custom fusion | bytes 12583936 | tf_op jit(solution)/shard_map/scatter | solution.py:91
  94.7 106.0 %collective-permute-done.2 = bf16[2,24,4,256]{3,2,1,0:T(4,128)(2,1)} collective-permute-done((bf16[2,24,4,256]{3,2,1,0:T(4,128)(2,1)}, bf16[2,24,4,256]{3,2,1,0:T(4,128)(2,1)}, u32[]{:S(2)}, u32[]{:S(2)}) %collective-permute-start.2) | collective-permute-done | bytes 98336 | tf_op jit(solution)/shard_map/ppermute | solution.py:15
  203.8 9.5 pad_maximum_fusion
  213.4 23.3 %all-to-all-done.1 = bf16[32,8,64,256]{3,2,1,0:T(8,128)(2,1)} async-done(((bf16[32,8,64,256]{3,2,1,0:T(8,128)(2,1)}), bf16[32,8,64,256]{3,2,1,0:T(8,128)(2,1)}, u32[]{:S(2)}, u32[]{:S(2)}) %all-to-all-start.1) | async-done | bytes 8388640 | tf_op jit(solution)/shard_map/all_to_all | solution.py:130
  236.6 841.3 %while.15 = (s32[]{:T(128)}, f32[8,32,5184]{2,1,0:T(8,128)}, s32[8,32]{1,0:T(8,128)S(1)}, bf16[8,32,64,256]{3,2,1,0:T(8,128)(2,1)}, bf16[2,24,40,256]{3,0,2,1:T(...) while((s32[]{:T(128)}, f32[8,32,5184]{2,1,0:T(8,128)}, ...), condition=%wide.region_6.7_spmd.clone.clone, body=%wide.region_5.6_spmd.clone.clone.sunk | while | flops 271506336 | bytes 39352320 | solution.py:142
  252.3 14.3 %gather_fusion = bf16[32,16,16,256]{3,0,2,1:T(8,128)(2,1)} fusion(bf16[2,40,72,256]{3,0,2,1:T(2,128)(2,1)} %get-tuple-element.338, s32[32]{0:T(128)S(1)} %fusion.53), kind=kCustom, calls=%fused_computation.1.clone.clone.1 | custom fusion | bytes 8389120 | tf_op jit(solution)/shard_map/while/body/eval_jaxpr/vmap()/gather | solution.py:104
  289.1 60.7 %gather_fusion.2 = f32[5184,32]{1,0:T(8,128)} fusion(f32[32,64,256]{0,2,1:T(8,128)} %copy.63, s32[5184]{0:T(1024)S(1)} %reshape.728), kind=kCustom, calls=%fused_computation.2.clone.clone.1 | custom fusion | bytes 1368576 | tf_op jit(solution)/shard_map/while/body/eval_jaxpr/vmap(jit(take_along_axis))/gather | solution.py:124
  355.7 14.1 %gather_fusion = bf16[32,16,16,256]{3,0,2,1:T(8,128)(2,1)} fusion(bf16[2,40,72,256]{3,0,2,1:T(2,128)(2,1)} %get-tuple-element.338, s32[32]{0:T(128)S(1)} %fusion.53), kind=kCustom, calls=%fused_computation.1.clone.clone.1 | custom fusion | bytes 8389120 | tf_op jit(solution)/shard_map/while/body/eval_jaxpr/vmap()/gather | solution.py:104
  392.3 60.7 %gather_fusion.2 = f32[5184,32]{1,0:T(8,128)} fusion(f32[32,64,256]{0,2,1:T(8,128)} %copy.63, s32[5184]{0:T(1024)S(1)} %reshape.728), kind=kCustom, calls=%fused_computation.2.clone.clone.1 | custom fusion | bytes 1368576 | tf_op jit(solution)/shard_map/while/body/eval_jaxpr/vmap(jit(take_along_axis))/gather | solution.py:124
  458.8 13.8 %gather_fusion = bf16[32,16,16,256]{3,0,2,1:T(8,128)(2,1)} fusion(bf16[2,40,72,256]{3,0,2,1:T(2,128)(2,1)} %get-tuple-element.338, s32[32]{0:T(128)S(1)} %fusion.53), kind=kCustom, calls=%fused_computation.1.clone.clone.1 | custom fusion | bytes 8389120 | tf_op jit(solution)/shard_map/while/body/eval_jaxpr/vmap()/gather | solution.py:104
  495.2 60.7 %gather_fusion.2 = f32[5184,32]{1,0:T(8,128)} fusion(f32[32,64,256]{0,2,1:T(8,128)} %copy.63, s32[5184]{0:T(1024)S(1)} %reshape.728), kind=kCustom, calls=%fused_computation.2.clone.clone.1 | custom fusion | bytes 1368576 | tf_op jit(solution)/shard_map/while/body/eval_jaxpr/vmap(jit(take_along_axis))/gather | solution.py:124
  561.7 14.3 %gather_fusion = bf16[32,16,16,256]{3,0,2,1:T(8,128)(2,1)} fusion(bf16[2,40,72,256]{3,0,2,1:T(2,128)(2,1)} %get-tuple-element.338, s32[32]{0:T(128)S(1)} %fusion.53), kind=kCustom, calls=%fused_computation.1.clone.clone.1 | custom fusion | bytes 8389120 | tf_op jit(solution)/shard_map/while/body/eval_jaxpr/vmap()/gather | solution.py:104
  598.5 60.7 %gather_fusion.2 = f32[5184,32]{1,0:T(8,128)} fusion(f32[32,64,256]{0,2,1:T(8,128)} %copy.63, s32[5184]{0:T(1024)S(1)} %reshape.728), kind=kCustom, calls=%fused_computation.2.clone.clone.1 | custom fusion | bytes 1368576 | tf_op jit(solution)/shard_map/while/body/eval_jaxpr/vmap(jit(take_along_axis))/gather | solution.py:124
  665.1 13.9 %gather_fusion = bf16[32,16,16,256]{3,0,2,1:T(8,128)(2,1)} fusion(bf16[2,40,72,256]{3,0,2,1:T(2,128)(2,1)} %get-tuple-element.338, s32[32]{0:T(128)S(1)} %fusion.53), kind=kCustom, calls=%fused_computation.1.clone.clone.1 | custom fusion | bytes 8389120 | tf_op jit(solution)/shard_map/while/body/eval_jaxpr/vmap()/gather | solution.py:104
  701.5 60.7 %gather_fusion.2 = f32[5184,32]{1,0:T(8,128)} fusion(f32[32,64,256]{0,2,1:T(8,128)} %copy.63, s32[5184]{0:T(1024)S(1)} %reshape.728), kind=kCustom, calls=%fused_computation.2.clone.clone.1 | custom fusion | bytes 1368576 | tf_op jit(solution)/shard_map/while/body/eval_jaxpr/vmap(jit(take_along_axis))/gather | solution.py:124
  768.0 14.2 %gather_fusion = bf16[32,16,16,256]{3,0,2,1:T(8,128)(2,1)} fusion(bf16[2,40,72,256]{3,0,2,1:T(2,128)(2,1)} %get-tuple-element.338, s32[32]{0:T(128)S(1)} %fusion.53), kind=kCustom, calls=%fused_computation.1.clone.clone.1 | custom fusion | bytes 8389120 | tf_op jit(solution)/shard_map/while/body/eval_jaxpr/vmap()/gather | solution.py:104
  804.8 60.7 %gather_fusion.2 = f32[5184,32]{1,0:T(8,128)} fusion(f32[32,64,256]{0,2,1:T(8,128)} %copy.63, s32[5184]{0:T(1024)S(1)} %reshape.728), kind=kCustom, calls=%fused_computation.2.clone.clone.1 | custom fusion | bytes 1368576 | tf_op jit(solution)/shard_map/while/body/eval_jaxpr/vmap(jit(take_along_axis))/gather | solution.py:124
  871.3 14.2 %gather_fusion = bf16[32,16,16,256]{3,0,2,1:T(8,128)(2,1)} fusion(bf16[2,40,72,256]{3,0,2,1:T(2,128)(2,1)} %get-tuple-element.338, s32[32]{0:T(128)S(1)} %fusion.53), kind=kCustom, calls=%fused_computation.1.clone.clone.1 | custom fusion | bytes 8389120 | tf_op jit(solution)/shard_map/while/body/eval_jaxpr/vmap()/gather | solution.py:104
  908.1 60.7 %gather_fusion.2 = f32[5184,32]{1,0:T(8,128)} fusion(f32[32,64,256]{0,2,1:T(8,128)} %copy.63, s32[5184]{0:T(1024)S(1)} %reshape.728), kind=kCustom, calls=%fused_computation.2.clone.clone.1 | custom fusion | bytes 1368576 | tf_op jit(solution)/shard_map/while/body/eval_jaxpr/vmap(jit(take_along_axis))/gather | solution.py:124
  974.6 14.1 %gather_fusion = bf16[32,16,16,256]{3,0,2,1:T(8,128)(2,1)} fusion(bf16[2,40,72,256]{3,0,2,1:T(2,128)(2,1)} %get-tuple-element.338, s32[32]{0:T(128)S(1)} %fusion.53), kind=kCustom, calls=%fused_computation.1.clone.clone.1 | custom fusion | bytes 8389120 | tf_op jit(solution)/shard_map/while/body/eval_jaxpr/vmap()/gather | solution.py:104
  1011.3 60.7 %gather_fusion.2 = f32[5184,32]{1,0:T(8,128)} fusion(f32[32,64,256]{0,2,1:T(8,128)} %copy.63, s32[5184]{0:T(1024)S(1)} %reshape.728), kind=kCustom, calls=%fused_computation.2.clone.clone.1 | custom fusion | bytes 1368576 | tf_op jit(solution)/shard_map/while/body/eval_jaxpr/vmap(jit(take_along_axis))/gather | solution.py:124
  1077.9 9.6 all_to_all.20
  1087.5 150.5 %all_to_all.24 = f32[32,1,41472]{2,1,0:T(1,128)} all-to-all(f32[32,1,41472]{2,1,0:T(1,128)} %all_to_all.20), channel_id=1, replica_groups=mesh['rows'=8,'cols'=4] {'rows','cols'}, dimensions={0} | all-to-all | bytes 10616832 | tf_op jit(solution)/shard_map/all_to_all | solution.py:151
  1238.0 56.4 %reduce.2 = f32[32,41472]{1,0:T(8,128)} reduce(f32[32,1,41472]{2,1,0:T(1,128)} %all_to_all.24, f32[]{:T(128)} %constant.471), dimensions={1}, to_apply=%all_to_all.19.reduce_sub_computation | reduce | bytes 10616836 | tf_op jit(solution)/shard_map/all_to_all | solution.py:151
  (196 shorter events, 328.3 us)
Async XLA Ops:
  12.4 36.7 %all-to-all-start = ((s32[32,1,8]{2,1,0:T(1,128)}), s32[32,1,8]{2,1,0:T(1,128)S(1)}, u32[]{:S(2)}, u32[]{:S(2)}) async-start(s32[32,1,8]{2,1,0:T(1,128)} %copy.35), calls=%async_computation | async-start | bytes 32768 | tf_op jit(solution)/shard_map/all_to_all | solution.py:133
  49.1 6.0 copy-start
  49.1 187.6 %all-to-all-start.1 = ((bf16[32,8,64,256]{3,2,1,0:T(8,128)(2,1)}), bf16[32,8,64,256]{3,2,1,0:T(8,128)(2,1)}, u32[]{:S(2)}, u32[]{:S(2)}) async-start(bf16[32,8,64,256]{3,2,1,0:T(8,128)(2,1)} %scatter_fusion.1), calls=%async_computation.1 | async-start | bytes 16777216 | tf_op jit(solution)/shard_map/all_to_all | solution.py:130
  55.4 26.3 %collective-permute-start.4 = (bf16[2,4,64,256]{3,0,2,1:T(2,128)(2,1)S(1)}, bf16[2,4,64,256]{3,0,2,1:T(2,128)(2,1)}, u32[]{:S(2)}, u32[]{:S(2)}) collective-permute-start(bf16[2,4,64,256]{3,0,2,1:T(2,128)(2,1)S(1)} %copy.55), channel_id=1, source_target_pairs={{0,4},{4,8},{8,12},{12,16},{16,20},{20,24},{24,28},{1,5},{5,9},{9,... | collective-permute-start | bytes 786440 | tf_op jit(solution)/shard_map/ppermute | solution.py:15
  69.5 5.8 collective-permute-start
  72.4 3.2 collective-permute-start.1
  74.0 11.2 collective-permute-start.5
  76.4 124.2 %collective-permute-start.2 = (bf16[2,24,4,256]{3,2,1,0:T(4,128)(2,1)}, bf16[2,24,4,256]{3,2,1,0:T(4,128)(2,1)}, u32[]{:S(2)}, u32[]{:S(2)}) collective-permute-start(bf16[2,24,4,256]{3,2,1,0:T(4,128)(2,1)} %get-tuple-element.232), channel_id=1, source_target_pairs={{0,1},{1,2},{2,3},{4,5},{5,6},{6,7},{8,9},{9,10},{10,11},{12,13},{... | collective-permute-start | bytes 294920 | tf_op jit(solution)/shard_map/ppermute | solution.py:15
  80.4 120.2 %collective-permute-start.3 = (bf16[2,24,4,256]{3,2,1,0:T(4,128)(2,1)}, bf16[2,24,4,256]{3,2,1,0:T(4,128)(2,1)}, u32[]{:S(2)}, u32[]{:S(2)}) collective-permute-start(bf16[2,24,4,256]{3,2,1,0:T(4,128)(2,1)} %get-tuple-element.233), channel_id=1, source_target_pairs={{1,0},{2,1},{3,2},{5,4},{6,5},{7,6},{9,8},{10,9},{11,10},{13,12},{... | collective-permute-start | bytes 294920 | tf_op jit(solution)/shard_map/ppermute | solution.py:18
  85.4 1.5 copy-start.2
  87.8 116.0 %collective-permute-start.6 = (bf16[2,40,4,256]{3,0,2,1:T(2,128)(2,1)}, bf16[2,40,4,256]{3,0,2,1:T(2,128)(2,1)S(1)}, u32[]{:S(2)}, u32[]{:S(2)}) collective-permute-start(bf16[2,40,4,256]{3,0,2,1:T(2,128)(2,1)} %get-tuple-element.228), channel_id=1, source_target_pairs={{0,1},{1,2},{2,3},{4,5},{5,6},{6,7},{8,9},{9,10},{10,11},{12,13},{... | collective-permute-start | bytes 491528 | tf_op jit(solution)/shard_map/ppermute | solution.py:15
  92.3 111.5 %collective-permute-start.7 = (bf16[2,40,4,256]{3,0,2,1:T(2,128)(2,1)S(1)}, bf16[2,40,4,256]{3,0,2,1:T(2,128)(2,1)S(1)}, u32[]{:S(2)}, u32[]{:S(2)}) collective-permute-start(bf16[2,40,4,256]{3,0,2,1:T(2,128)(2,1)S(1)} %get-tuple-element.229), channel_id=1, source_target_pairs={{1,0},{2,1},{3,2},{5,4},{6,5},{7,6},{9,8},{10,9},{11,10},{13,12},{... | collective-permute-start | bytes 491528 | tf_op jit(solution)/shard_map/ppermute | solution.py:18
  94.7 109.2 %copy-start.3 = (bf16[2,40,64,256]{3,0,2,1:T(2,128)(2,1)S(1)}, bf16[2,40,64,256]{3,0,2,1:T(2,128)(2,1)}, u32[]{:S(2)}) copy-start(bf16[2,40,64,256]{3,0,2,1:T(2,128)(2,1)} %copy-done.2) | copy-start | bytes 7864324
  1294.5 6.2 copy-start.1
where the time goes:
time: 1330 us; the launch traced here: 1320 us
  local copies, waits for them, and re-layouts  830 us (62%)
  blocking collectives  151 us (11%)
  waiting for transfers between devices  130 us (10%)
  other arithmetic  91.2 us (7%)
  matrix products  67.3 us (5%)
  starting transfers between devices  32.9 us (2%)
  loops' own time  16.4 us (1%)
    gather x40, local copies, waits for them, and re-layouts, correlate(): correlation = jnp.take_along_axis(scores, window_ids, axis=1)  523 us
    gather x16, local copies, waits for them, and re-layouts, correlate(): lax.dynamic_slice(padded[level], (frame_id, tile_ids // level_across * ti...  186 us
    all_to_all x1, blocking collectives, body(): lax.all_to_all(replies.reshape(device_count, slot_count * row_width), ('r...  151 us
    ppermute x4, waiting for transfers between devices, padded_2(): lax.ppermute(lax.slice_in_dim(block, block.shape[dim] - width, None, axis...  107 us
    dot_general x8, matrix products, correlate(): jnp.einsum('qc,pc->qp', query_rows, target_cells.reshape(span_side * span...  67.3 us
    all_to_all x1, other arithmetic, body(): lax.all_to_all(replies.reshape(device_count, slot_count * row_width), ('r...  56.4 us
    mul x8, local copies, waits for them, and re-layouts, correlate(): jnp.einsum('qc,pc->qp', query_rows, target_cells.reshape(span_side * span...  37.4 us
  transfers between devices with their start and end apart: 10, of which 4 were waited for; matrix products, arithmetic and copies ran while one was open for 5% of the time, Pallas kernels for 0%

commit v1 on v0

v1 whole, which is shorter than its diff:
```python
import functools

import jax
import jax.numpy as jnp
from jax import lax
from jax.experimental import pallas as pl
from jax.experimental.pallas import tpu as pltpu
from jax.sharding import PartitionSpec as P

RADIUS = 4
LEVELS = 2


def padded_2(block, sides, width):
    for axis, dim in sides:
        count = lax.axis_size(axis)
        forward = [(i, i + 1) for i in range(count - 1)]
        backward = [(target, source) for source, target in forward]
        low = lax.ppermute(
            lax.slice_in_dim(block, block.shape[dim] - width, None, axis=dim), axis, forward
        )
        high = lax.ppermute(lax.slice_in_dim(block, 0, width, axis=dim), axis, backward)
        block = jnp.concatenate([low, block, high], axis=dim)
    return block


def pool_level(level_map):
    frame_count, rows_in, cols_in, channels = level_map.shape
    pooled = level_map.astype(jnp.float32).reshape(
        frame_count, rows_in // 2, 2, cols_in // 2, 2, channels
    )
    return jnp.mean(pooled, axis=(2, 4)).astype(jnp.bfloat16)


def dispatch_kernel(slot_count, block_ref, query_ref, sent_ref):
    base = pl.program_id(0) * slot_count
    for slot in range(slot_count):
        sent_ref[slot] = query_ref[block_ref[base + slot]]


def correlate_kernel(plan, scale, slot_count, label_ref, query_ref, *refs):
    map_refs, reply_ref = refs[:-1], refs[-1]
    per_frame, levels = plan
    tile_side = 2 * RADIUS
    span_side = 4 * RADIUS
    window_side = 2 * RADIUS + 1
    block_cells = tile_side * tile_side
    owner_slots = slot_count // LEVELS
    base = pl.program_id(0) * slot_count
    lane = lax.broadcasted_iota(jnp.int32, (1, 1, 2 * block_cells), 2)
    query_row = lane % block_cells // tile_side
    query_col = lane[0] % tile_side
    is_first = lane[0] < block_cells

    def window(slot):
        padded_rows, across = levels[slot // owner_slots]
        label = label_ref[base + slot]
        tile = label % per_frame
        row = label // per_frame * padded_rows + tile // across * tile_side
        col = pl.multiple_of(tile % across * tile_side, tile_side)
        cells = map_refs[slot // owner_slots][pl.ds(row, span_side), pl.ds(col, span_side), :]
        return cells.reshape(span_side * span_side, -1).astype(jnp.bfloat16)

    for pair in range(slot_count // 2):
        queries = query_ref[2 * pair : 2 * pair + 2].reshape(2 * block_cells, -1)
        first, second = [
            lax.dot_general(
                window(2 * pair + half),
                queries,
                (((1,), (1,)), ((), ())),
                preferred_element_type=jnp.float32,
            )
            for half in range(2)
        ]
        scores = jnp.where(is_first, first, second)
        scores = scores.reshape(span_side, span_side, 2 * block_cells)
        for bit in (1, 2, 4):
            scores = jnp.where((query_row & bit) != 0, scores[bit:], scores[:-bit])
        flat = scores.reshape(window_side * span_side, 2 * block_cells)
        for bit in (1, 2, 4):
            moved = pltpu.roll(flat, flat.shape[0] - bit, 0)
            flat = jnp.where((query_col & bit) != 0, moved, flat)
        flat = flat * scale
        for a in range(window_side):
            reply_ref[pair, a * window_side : (a + 1) * window_side, :] = flat[
                a * span_side : a * span_side + window_side
            ]


def assemble_kernel(pair_count, source_ref, half_ref, reply_ref, out_ref):
    lanes = reply_ref.shape[2]
    is_first = lax.broadcasted_iota(jnp.int32, reply_ref.shape[1:], 1) < lanes // 2
    for level in range(LEVELS):

        def step(m, carry, level=level):
            at = 2 * (level * pair_count + m)
            picked = []
            for side in range(2):
                rows = reply_ref[source_ref[at + side]]
                moved = pltpu.roll(rows, lanes // 2, 1)
                picked.append(jnp.where(half_ref[at + side] == side, rows, moved))
            spot = pl.ds(pl.multiple_of(m * lanes, lanes), lanes)
            out_ref[level, :, spot] = jnp.where(is_first, picked[0], picked[1])
            return carry

        lax.fori_loop(0, pair_count, step, 0)


def body(fmap1, fmap2, target_owner, target_tile):
    tile_side = 2 * RADIUS
    window_side = 2 * RADIUS + 1
    block_cells = tile_side * tile_side
    frame_count, band_rows, band_cols, channels = fmap1.shape
    device_count = lax.axis_size("rows") * lax.axis_size("cols")
    tiles_across = band_cols // tile_side
    per_frame = band_rows // tile_side * tiles_across
    block_count = frame_count * per_frame
    owner_slots = max(2, (2 * block_count + device_count - 1) // device_count)
    owner_slots += owner_slots % 2
    slot_count = LEVELS * owner_slots
    pair_slots = slot_count // 2
    queries = fmap1.reshape(
        frame_count, band_rows // tile_side, tile_side, tiles_across, tile_side, channels
    )
    queries = queries.transpose(0, 1, 3, 2, 4, 5).reshape(block_count, block_cells, channels)
    owner_ids = target_owner[:, :, 0]
    peer_ids = jnp.arange(device_count, dtype=jnp.int32)
    owner_hits = (owner_ids[:, :, None] == peer_ids[None, None, :]).astype(jnp.int32)
    slot_rank = jnp.sum(owner_hits * (jnp.cumsum(owner_hits, axis=1) - 1), axis=2)
    block_ids = jnp.arange(block_count, dtype=jnp.int32)
    label_rows = []
    for level in range(LEVELS):
        tile_count = (band_rows >> level) // tile_side * ((band_cols >> level) // tile_side)
        label_rows.append(block_ids // per_frame * per_frame + target_tile[level] % tile_count)
    rank_ids = jnp.arange(owner_slots, dtype=jnp.int32)
    rank_hits = (slot_rank[:, :, None] == rank_ids[None, None, :]).astype(jnp.int32)
    slot_hits = owner_hits[:, :, :, None] * rank_hits[:, :, None, :]

    def by_slot(values):
        table = jnp.sum(slot_hits * values[:, :, None, None], axis=1)
        return table.transpose(1, 0, 2).reshape(device_count, slot_count)

    labels_sent = by_slot(jnp.stack(label_rows))
    blocks_sent = by_slot(jnp.broadcast_to(block_ids[None], owner_ids.shape))
    slot_block = (slot_count, block_cells, channels)
    slot_total = device_count * slot_count
    queries_sent = pl.pallas_call(
        functools.partial(dispatch_kernel, slot_count),
        out_shape=jax.ShapeDtypeStruct((slot_total,) + slot_block[1:], jnp.bfloat16),
        grid_spec=pltpu.PrefetchScalarGridSpec(
            num_scalar_prefetch=1,
            grid=(device_count,),
            in_specs=[pl.BlockSpec(queries.shape, lambda d, *_: (0, 0, 0))],
            out_specs=pl.BlockSpec(slot_block, lambda d, *_: (d, 0, 0)),
        ),
    )(blocks_sent.reshape(-1), queries)
    label_part = lax.all_to_all(
        labels_sent, ("rows", "cols"), split_axis=0, concat_axis=0, tiled=True
    )
    query_part = lax.all_to_all(
        queries_sent.reshape((device_count,) + slot_block),
        ("rows", "cols"),
        split_axis=0,
        concat_axis=0,
        tiled=True,
    )
    levels = [fmap2]
    for level in range(1, LEVELS):
        levels.append(pool_level(levels[-1]))
    maps = []
    plan = []
    for level_map in levels:
        padded = padded_2(level_map, (("rows", 1), ("cols", 2)), RADIUS).astype(jnp.float32)
        maps.append(padded.reshape((-1,) + padded.shape[2:]))
        plan.append((padded.shape[1], level_map.shape[2] // tile_side))
    window_cells = window_side * window_side
    reply_block = (pair_slots, window_cells, 2 * block_cells)
    replies = pl.pallas_call(
        functools.partial(
            correlate_kernel, (per_frame, tuple(plan)), channels ** (-0.5), slot_count
        ),
        out_shape=jax.ShapeDtypeStruct(
            (device_count * pair_slots,) + reply_block[1:], jnp.float32
        ),
        grid_spec=pltpu.PrefetchScalarGridSpec(
            num_scalar_prefetch=1,
            grid=(device_count,),
            in_specs=[pl.BlockSpec(slot_block, lambda d, *_: (d, 0, 0))]
            + [pl.BlockSpec(level_map.shape, lambda d, *_: (0, 0, 0)) for level_map in maps],
            out_specs=pl.BlockSpec(reply_block, lambda d, *_: (d, 0, 0)),
        ),
    )(label_part.reshape(-1), query_part.reshape((slot_total,) + slot_block[1:]), *maps)
    returned = lax.all_to_all(
        replies.reshape((device_count,) + reply_block),
        ("rows", "cols"),
        split_axis=0,
        concat_axis=0,
        tiled=True,
    )
    level_ids = jnp.arange(LEVELS, dtype=jnp.int32)[:, None]
    slot_ids = level_ids * owner_slots + slot_rank
    source_ids = owner_ids * pair_slots + slot_ids // 2
    reply_table = returned.reshape((device_count * pair_slots,) + reply_block[1:])
    return pl.pallas_call(
        functools.partial(assemble_kernel, block_count // 2),
        out_shape=jax.ShapeDtypeStruct(
            (LEVELS, window_cells, block_count * block_cells), jnp.float32
        ),
        in_specs=[
            pl.BlockSpec(memory_space=pltpu.SMEM),
            pl.BlockSpec(memory_space=pltpu.SMEM),
            pl.BlockSpec(memory_space=pltpu.VMEM),
        ],
        out_specs=pl.BlockSpec(memory_space=pltpu.VMEM),
    )(source_ids.reshape(-1), (slot_ids % 2).reshape(-1), reply_table)


def solution(mesh):
    in_specs = (
        P(None, "rows", "cols", None),
        P(None, "rows", "cols", None),
        P(None, ("rows", "cols"), None),
        P(None, ("rows", "cols")),
    )
    out_specs = P(None, None, ("rows", "cols"))
    return jax.shard_map(body, mesh=mesh, in_specs=in_specs, out_specs=out_specs, check_vma=False)
```

time: 1330 us -> 408 us (0.31)
  local copies, waits for them, and re-layouts: 830 us -> 28.8 us
  blocking collectives: 151 us -> 0 us
  waiting for transfers between devices: 130 us -> 257 us
  other arithmetic: 91.2 us -> 15.1 us
  matrix products: 67.3 us -> 0 us
  Pallas kernels: 0 us -> 52.5 us
  starting transfers between devices: 32.9 us -> 51.3 us
  loops' own time: 16.4 us -> 0 us
    gather x57 -> x0, local copies, waits for them, and re-layouts: 713 us -> none  [the longest x40 523 us: correlate(): correlation = jnp.take_along_axis(scores, window_ids, axis=1)]
    all_to_all x1 -> x0, blocking collectives: 151 us -> none  [body(): lax.all_to_all(replies.reshape(device_count, slot_count * row_width), ('r...]
    all_to_all x1 -> x2, waiting for transfers between devices: 23.3 us -> 144 us  [the longest x1 115 us: body(): lax.all_to_all(replies.reshape((device_count,) + reply_block), ('rows', '...]
    dot_general x8 -> x0, matrix products: 67.3 us -> none  [correlate(): jnp.einsum('qc,pc->qp', query_rows, target_cells.reshape(span_side * span...]
    ppermute x4, waiting for transfers between devices: 0.34 us -> 60.4 us  [padded_2(): lax.ppermute(lax.slice_in_dim(block, 0, width, axis=dim), axis, backward)]
    all_to_all x1 -> x0, other arithmetic: 56.4 us -> none  [body(): lax.all_to_all(replies.reshape(device_count, slot_count * row_width), ('r...]
    ppermute x4, waiting for transfers between devices: 107 us -> 52.8 us  [padded_2(): lax.ppermute(lax.slice_in_dim(block, block.shape[dim] - width, None, axis...]
    pallas_call x0 -> x3, Pallas kernels: none -> 52.5 us  [the longest x1 28.3 us: body(): pl.pallas_call(functools.partial(correlate_kernel, (per_frame, tuple(plan...]
  transfers between devices with their start and end apart: 10 -> 11, of which waited for: 4 -> 5; matrix products, arithmetic and copies ran while one was open for 5% -> 5% of each run, Pallas kernels for 0% -> 3%
where the time goes in v1:
time: 408 us; the launch traced here: 405 us
  waiting for transfers between devices  257 us (63%)
  Pallas kernels  52.5 us (13%)
  starting transfers between devices  51.3 us (13%)
  local copies, waits for them, and re-layouts  28.8 us (7%)
  other arithmetic  15.1 us (4%)
    all_to_all x1, waiting for transfers between devices, body(): lax.all_to_all(replies.reshape((device_count,) + reply_block), ('rows', '...  115 us
    ppermute x4, waiting for transfers between devices, padded_2(): lax.ppermute(lax.slice_in_dim(block, 0, width, axis=dim), axis, backward)  60.4 us
    ppermute x4, waiting for transfers between devices, padded_2(): lax.ppermute(lax.slice_in_dim(block, block.shape[dim] - width, None, axis...  52.8 us
    all_to_all x1, waiting for transfers between devices, body(): lax.all_to_all(queries_sent.reshape((device_count,) + slot_block), ('rows...  29.2 us
    pallas_call x1, Pallas kernels, body(): pl.pallas_call(functools.partial(correlate_kernel, (per_frame, tuple(plan...  28.3 us
    all_to_all x1, starting transfers between devices, body(): lax.all_to_all(replies.reshape((device_count,) + reply_block), ('rows', '...  17.4 us
    ppermute x4, starting transfers between devices, padded_2(): lax.ppermute(lax.slice_in_dim(block, block.shape[dim] - width, None, axis...  15.5 us
    pallas_call x1, Pallas kernels, body(): pl.pallas_call(functools.partial(dispatch_kernel, slot_count), out_shape=...  14 us
  transfers between devices with their start and end apart: 11, of which 5 were waited for; matrix products, arithmetic and copies ran while one was open for 5% of the time, Pallas kernels for 3%

profile of v1, /device:TPU:0, one launch (start us, length us, event | category | flops | bytes accessed | tf_op | source)
XLA Modules:
  0.0 405.1 jit_solution(10656912504757367497)
XLA Ops:
  3.6 7.3 %all-to-all-start = ((s32[32,1,8]{2,1,0:T(1,128)}), s32[32,1,8]{2,1,0:T(1,128)S(1)}, u32[]{:S(2)}, u32[]{:S(2)}) async-start(s32[32,1,8]{2,1,0:T(1,128)} %copy.16), calls=%async_computation | async-start | bytes 32768 | tf_op jit(solution)/shard_map/all_to_all | solution.py:157
  11.8 3.2 copy.18
  15.0 14.0 %shard_map.46 = bf16[256,64,256]{2,1,0:T(8,128)(2,1)} custom-call(s32[256]{0:T(256)} %reshape_reshape.3.block_ref, bf16[64,64,256]{2,1,0:T(8,128)(2,1)} %bitcast.24), custom_call_target="tpu_custom_call" | custom-call | tf_op jit(solution)/shard_map/pallas_call | solution.py:147
  29.0 6.0 %all-to-all-start.1 = ((bf16[32,8,64,256]{3,2,1,0:T(8,128)(2,1)}), bf16[32,8,64,256]{3,2,1,0:T(8,128)(2,1)}, u32[]{:S(2)}, u32[]{:S(2)}) async-start(bf16[32,8,64,256]{3,2,1,0:T(8,128)(2,1)} %bitcast.21), calls=%async_computation.1 | async-start | bytes 16777216 | tf_op jit(solution)/shard_map/all_to_all | solution.py:160
  35.0 3.5 reshape.113
  38.5 5.5 %reduce_sum.39 = f32[2,16,32,256]{3,2,1,0:T(8,128)S(1)} reduce(f32[2,16,2,32,2,256]{5,4,3,2,1,0:T(2,128)} %reshape.113, f32[]{:T(128)} %constant.82.clone.1), dimensions={2,4}, to_apply=%region_4.5 | reduce | flops 786432 | bytes 5242884 | tf_op jit(solution)/shard_map/reduce_sum | solution.py:32
  45.4 3.0 collective-permute-start.4
  48.5 3.3 collective-permute-start
  54.7 4.6 %collective-permute-start.6 = (bf16[2,24,4,256]{3,2,1,0:T(4,128)(2,1)S(1)}, bf16[2,24,4,256]{3,2,1,0:T(4,128)(2,1)S(1)}, u32[]{:S(2)}, u32[]{:S(2)}) collective-permute-start(bf16[2,24,4,256]{3,2,1,0:T(4,128)(2,1)S(1)} %get-tuple-element.11), channel_id=1, source_target_pairs={{0,1},{1,2},{2,3},{4,5},{5,6},{6,7},{8,9},{9,10},{10,11},{12,13},{... | collective-permute-start | bytes 294920 | tf_op jit(solution)/shard_map/ppermute | solution.py:19
  59.5 1.5 copy-done.1
  62.4 4.6 %collective-permute-start.2 = (bf16[2,40,4,256]{3,2,1,0:T(4,128)(2,1)S(1)}, bf16[2,40,4,256]{3,2,1,0:T(4,128)(2,1)S(1)}, u32[]{:S(2)}, u32[]{:S(2)}) collective-permute-start(bf16[2,40,4,256]{3,2,1,0:T(4,128)(2,1)S(1)} %get-tuple-element.7), channel_id=1, source_target_pairs={{0,1},{1,2},{2,3},{4,5},{5,6},{6,7},{8,9},{9,10},{10,11},{12,13},{... | collective-permute-start | bytes 491528 | tf_op jit(solution)/shard_map/ppermute | solution.py:19
  68.8 60.4 %collective-permute-done.7 = bf16[2,24,4,256]{3,2,1,0:T(4,128)(2,1)S(1)} collective-permute-done((bf16[2,24,4,256]{3,2,1,0:T(4,128)(2,1)S(1)}, bf16[2,24,4,256]{3,2,1,0:T(4,128)(2,1)S(1)}, u32[]{:S(2)}, u32[]{:S(2)}) %collective-permute-start.7) | collective-permute-done | bytes 98336 | tf_op jit(solution)/shard_map/ppermute | solution.py:22
  129.2 51.2 %collective-permute-done.6 = bf16[2,24,4,256]{3,2,1,0:T(4,128)(2,1)S(1)} collective-permute-done((bf16[2,24,4,256]{3,2,1,0:T(4,128)(2,1)S(1)}, bf16[2,24,4,256]{3,2,1,0:T(4,128)(2,1)S(1)}, u32[]{:S(2)}, u32[]{:S(2)}) %collective-permute-start.6) | collective-permute-done | bytes 98336 | tf_op jit(solution)/shard_map/ppermute | solution.py:19
  180.4 1.6 maximum_convert_fusion.1.refs_1_
  182.1 1.6 collective-permute-done.2
  183.6 3.7 maximum_convert_fusion.refs_0_
  187.3 29.2 %all-to-all-done.1 = bf16[32,8,64,256]{3,2,1,0:T(8,128)(2,1)} async-done(((bf16[32,8,64,256]{3,2,1,0:T(8,128)(2,1)}), bf16[32,8,64,256]{3,2,1,0:T(8,128)(2,1)}, u32[]{:S(2)}, u32[]{:S(2)}) %all-to-all-start.1) | async-done | bytes 8388640 | tf_op jit(solution)/shard_map/all_to_all | solution.py:160
  216.5 28.3 %shard_map.47 = f32[128,81,128]{2,1,0:T(8,128)} custom-call(s32[256]{0:T(256)} %reshape.103.label_ref, bf16[256,64,256]{2,1,0:T(8,128)(2,1)} %bitcast.8.query_ref, f32[80,72,256]{2,1,0:T(8,128)} %maximum_convert_fusion.refs_0_, f32[48,40,256]{2,1,0:T(8,128)} %maximum_convert_fusion.1.refs_1_), custom_call_target="tpu_custom_call" | custom-call | tf_op jit(solution)/shard_map/pallas_call | solution.py:178
  244.8 6.3 %copy.19 = f32[32,4,81,128]{3,1,2,0:T(4,128)} copy(f32[32,4,81,128]{3,2,1,0:T(8,128)} %bitcast.23) | data formatting | bytes 10616832 | tf_op jit(solution)/shard_map/reshape | solution.py:194
  251.1 17.4 %all-to-all-start.2 = ((f32[32,4,81,128]{3,1,2,0:T(4,128)}), f32[32,4,81,128]{3,1,2,0:T(4,128)}, u32[]{:S(2)}, u32[]{:S(2)}) async-start(f32[32,4,81,128]{3,1,2,0:T(4,128)} %copy.19), calls=%async_computation.2 | async-start | bytes 10616832 | tf_op jit(solution)/shard_map/all_to_all | solution.py:193
  269.3 114.8 %all-to-all-done.2 = f32[32,4,81,128]{3,1,2,0:T(4,128)} async-done(((f32[32,4,81,128]{3,1,2,0:T(4,128)}), f32[32,4,81,128]{3,1,2,0:T(4,128)}, u32[]{:S(2)}, u32[]{:S(2)}) %all-to-all-start.2) | async-done | bytes 5308448 | tf_op jit(solution)/shard_map/all_to_all | solution.py:193
  384.0 5.5 %copy.20 = f32[32,4,81,128]{3,2,1,0:T(8,128)} copy(f32[32,4,81,128]{3,1,2,0:T(4,128)} %all-to-all-done.2) | data formatting | bytes 10616832 | tf_op jit(solution)/shard_map/all_to_all | solution.py:193
  389.5 10.2 %shard_map.48 = f32[2,81,4096]{2,1,0:T(8,128)} custom-call(s32[128]{0:T(128)} %get-tuple-element.18.source_ref, s32[128]{0:T(128)} %get-tuple-element.17.half_ref, f32[128,81,128]{2,1,0:T(8,128)} %bitcast.22), custom_call_target="tpu_custom_call" | custom-call | tf_op jit(solution)/shard_map/pallas_call | solution.py:204
  399.7 5.4 %copy.21 = f32[2,81,4096]{2,0,1:T(2,128)} copy(f32[2,81,4096]{2,1,0:T(8,128)} %shard_map.48) | data formatting | bytes 5308416 | tf_op jit(solution)/shard_map/pallas_call | solution.py:204
  (46 shorter events, 12.9 us)
Async XLA Ops:
  3.6 25.4 %all-to-all-start = ((s32[32,1,8]{2,1,0:T(1,128)}), s32[32,1,8]{2,1,0:T(1,128)S(1)}, u32[]{:S(2)}, u32[]{:S(2)}) async-start(s32[32,1,8]{2,1,0:T(1,128)} %copy.16), calls=%async_computation | async-start | bytes 32768 | tf_op jit(solution)/shard_map/all_to_all | solution.py:157
  29.0 6.0 %copy-start = (bf16[2,32,64,256]{3,2,1,0:T(8,128)(2,1)S(1)}, bf16[2,32,64,256]{3,2,1,0:T(8,128)(2,1)}, u32[]{:S(2)}) copy-start(bf16[2,32,64,256]{3,2,1,0:T(8,128)(2,1)} %param.5) | copy-start | bytes 6291460
  29.0 187.5 %all-to-all-start.1 = ((bf16[32,8,64,256]{3,2,1,0:T(8,128)(2,1)}), bf16[32,8,64,256]{3,2,1,0:T(8,128)(2,1)}, u32[]{:S(2)}, u32[]{:S(2)}) async-start(bf16[32,8,64,256]{3,2,1,0:T(8,128)(2,1)} %bitcast.21), calls=%async_computation.1 | async-start | bytes 16777216 | tf_op jit(solution)/shard_map/all_to_all | solution.py:160
  44.1 9.0 %collective-permute-start.5 = (bf16[2,4,32,256]{3,2,1,0:T(8,128)(2,1)S(1)}, bf16[2,4,32,256]{3,2,1,0:T(8,128)(2,1)S(1)}, u32[]{:S(2)}, u32[]{:S(2)}) collective-permute-start(bf16[2,4,32,256]{3,2,1,0:T(8,128)(2,1)S(1)} %get-tuple-element.14), channel_id=1, source_target_pairs={{4,0},{8,4},{12,8},{16,12},{20,16},{24,20},{28,24},{5,1},{9,5},{13... | collective-permute-start | bytes 393224 | tf_op jit(solution)/shard_map/ppermute | solution.py:22
  45.4 7.7 %collective-permute-start.4 = (bf16[2,4,32,256]{3,2,1,0:T(8,128)(2,1)S(1)}, bf16[2,4,32,256]{3,2,1,0:T(8,128)(2,1)S(1)}, u32[]{:S(2)}, u32[]{:S(2)}) collective-permute-start(bf16[2,4,32,256]{3,2,1,0:T(8,128)(2,1)S(1)} %get-tuple-element.13), channel_id=1, source_target_pairs={{0,4},{4,8},{8,12},{12,16},{16,20},{20,24},{24,28},{1,5},{5,9},{9,... | collective-permute-start | bytes 393224 | tf_op jit(solution)/shard_map/ppermute | solution.py:19
  48.5 10.7 %collective-permute-start = (bf16[2,4,64,256]{3,2,1,0:T(8,128)(2,1)S(1)}, bf16[2,4,64,256]{3,2,1,0:T(8,128)(2,1)S(1)}, u32[]{:S(2)}, u32[]{:S(2)}) collective-permute-start(bf16[2,4,64,256]{3,2,1,0:T(8,128)(2,1)S(1)} %get-tuple-element.10), channel_id=1, source_target_pairs={{0,4},{4,8},{8,12},{12,16},{16,20},{20,24},{24,28},{1,5},{5,9},{9,... | collective-permute-start | bytes 786440 | tf_op jit(solution)/shard_map/ppermute | solution.py:19
  51.9 7.6 %collective-permute-start.1 = (bf16[2,4,64,256]{3,2,1,0:T(8,128)(2,1)S(1)}, bf16[2,4,64,256]{3,2,1,0:T(8,128)(2,1)S(1)}, u32[]{:S(2)}, u32[]{:S(2)}) collective-permute-start(bf16[2,4,64,256]{3,2,1,0:T(8,128)(2,1)S(1)} %get-tuple-element.9), channel_id=1, source_target_pairs={{4,0},{8,4},{12,8},{16,12},{20,16},{24,20},{28,24},{5,1},{9,5},{13... | collective-permute-start | bytes 786440 | tf_op jit(solution)/shard_map/ppermute | solution.py:22
  53.4 75.9 %collective-permute-start.7 = (bf16[2,24,4,256]{3,2,1,0:T(4,128)(2,1)S(1)}, bf16[2,24,4,256]{3,2,1,0:T(4,128)(2,1)S(1)}, u32[]{:S(2)}, u32[]{:S(2)}) collective-permute-start(bf16[2,24,4,256]{3,2,1,0:T(4,128)(2,1)S(1)} %get-tuple-element.12), channel_id=1, source_target_pairs={{1,0},{2,1},{3,2},{5,4},{6,5},{7,6},{9,8},{10,9},{11,10},{13,12},{... | collective-permute-start | bytes 294920 | tf_op jit(solution)/shard_map/ppermute | solution.py:22
  54.7 125.8 %collective-permute-start.6 = (bf16[2,24,4,256]{3,2,1,0:T(4,128)(2,1)S(1)}, bf16[2,24,4,256]{3,2,1,0:T(4,128)(2,1)S(1)}, u32[]{:S(2)}, u32[]{:S(2)}) collective-permute-start(bf16[2,24,4,256]{3,2,1,0:T(4,128)(2,1)S(1)} %get-tuple-element.11), channel_id=1, source_target_pairs={{0,1},{1,2},{2,3},{4,5},{5,6},{6,7},{8,9},{9,10},{10,11},{12,13},{... | collective-permute-start | bytes 294920 | tf_op jit(solution)/shard_map/ppermute | solution.py:19
  59.5 1.5 copy-start.1
  61.1 121.0 %collective-permute-start.3 = (bf16[2,40,4,256]{3,2,1,0:T(4,128)(2,1)S(1)}, bf16[2,40,4,256]{3,2,1,0:T(4,128)(2,1)S(1)}, u32[]{:S(2)}, u32[]{:S(2)}) collective-permute-start(bf16[2,40,4,256]{3,2,1,0:T(4,128)(2,1)S(1)} %get-tuple-element.8), channel_id=1, source_target_pairs={{1,0},{2,1},{3,2},{5,4},{6,5},{7,6},{9,8},{10,9},{11,10},{13,12},{... | collective-permute-start | bytes 491528 | tf_op jit(solution)/shard_map/ppermute | solution.py:22
  62.4 121.3 %collective-permute-start.2 = (bf16[2,40,4,256]{3,2,1,0:T(4,128)(2,1)S(1)}, bf16[2,40,4,256]{3,2,1,0:T(4,128)(2,1)S(1)}, u32[]{:S(2)}, u32[]{:S(2)}) collective-permute-start(bf16[2,40,4,256]{3,2,1,0:T(4,128)(2,1)S(1)} %get-tuple-element.7), channel_id=1, source_target_pairs={{0,1},{1,2},{2,3},{4,5},{5,6},{6,7},{8,9},{9,10},{10,11},{12,13},{... | collective-permute-start | bytes 491528 | tf_op jit(solution)/shard_map/ppermute | solution.py:19
  68.8 114.8 %copy-start.2 = (bf16[2,40,64,256]{3,2,1,0:T(8,128)(2,1)S(1)}, bf16[2,40,64,256]{3,2,1,0:T(8,128)(2,1)}, u32[]{:S(2)}) copy-start(bf16[2,40,64,256]{3,2,1,0:T(8,128)(2,1)} %copy-done.1) | copy-start | bytes 7864324
  251.1 17.5 %copy-start.3 = (s32[2,64,1]{1,2,0:T(1,128)S(1)}, s32[2,64,1]{1,2,0:T(1,128)}, u32[]{:S(2)}) copy-start(s32[2,64,1]{1,2,0:T(1,128)} %param.6) | copy-start | bytes 1540
  251.1 132.9 %all-to-all-start.2 = ((f32[32,4,81,128]{3,1,2,0:T(4,128)}), f32[32,4,81,128]{3,1,2,0:T(4,128)}, u32[]{:S(2)}, u32[]{:S(2)}) async-start(f32[32,4,81,128]{3,1,2,0:T(4,128)} %copy.19), calls=%async_computation.2 | async-start | bytes 10616832 | tf_op jit(solution)/shard_map/all_to_all | solution.py:193

commit v2 on v1

--- a/solution.py
+++ b/solution.py
@@ -9,6 +9,7 @@
 
 RADIUS = 4
 LEVELS = 2
+STEP_SLOTS = 16
 
 
 def padded_2(block, sides, width):
@@ -39,29 +40,56 @@
 
 
 def correlate_kernel(plan, scale, slot_count, label_ref, query_ref, *refs):
-    map_refs, reply_ref = refs[:-1], refs[-1]
-    per_frame, levels = plan
+    map_refs, (reply_ref, held, arrived) = refs[:-3], refs[-3:]
+    per_frame, col_count, levels = plan
     tile_side = 2 * RADIUS
     span_side = 4 * RADIUS
     window_side = 2 * RADIUS + 1
     block_cells = tile_side * tile_side
-    owner_slots = slot_count // LEVELS
-    base = pl.program_id(0) * slot_count
+    step = pl.program_id(0)
+    step_count = pl.num_programs(0)
+    level_steps = slot_count // LEVELS // STEP_SLOTS
     lane = lax.broadcasted_iota(jnp.int32, (1, 1, 2 * block_cells), 2)
     query_row = lane % block_cells // tile_side
     query_col = lane[0] % tile_side
     is_first = lane[0] < block_cells
 
+    def copy_of(at, slot, level):
+        padded_rows, across = levels[level]
+        label = label_ref[at * STEP_SLOTS + slot]
+        tile = label % per_frame
+        region = label // per_frame
+        row = region // col_count * padded_rows + tile // across * tile_side
+        col = (region % col_count * across + tile % across) * tile_side
+        col = pl.multiple_of(col, tile_side)
+        return pltpu.make_async_copy(
+            map_refs[level].at[pl.ds(row, span_side), pl.ds(col, span_side), :],
+            held.at[at % 2, slot],
+            arrived.at[at % 2, slot],
+        )
+
+    def fetch(at):
+        for level in range(LEVELS):
+
+            @pl.when(at // level_steps % LEVELS == level)
+            def _(level=level):
+                for slot in range(STEP_SLOTS):
+                    copy_of(at, slot, level).start()
+
+    @pl.when(step == 0)
+    def _():
+        fetch(step)
+
+    @pl.when(step + 1 < step_count)
+    def _():
+        fetch(step + 1)
+
     def window(slot):
-        padded_rows, across = levels[slot // owner_slots]
-        label = label_ref[base + slot]
-        tile = label % per_frame
-        row = label // per_frame * padded_rows + tile // across * tile_side
-        col = pl.multiple_of(tile % across * tile_side, tile_side)
-        cells = map_refs[slot // owner_slots][pl.ds(row, span_side), pl.ds(col, span_side), :]
+        copy_of(step, slot, 0).wait()
+        cells = held[step % 2, slot]
         return cells.reshape(span_side * span_side, -1).astype(jnp.bfloat16)
 
-    for pair in range(slot_count // 2):
+    for pair in range(STEP_SLOTS // 2):
         queries = query_ref[2 * pair : 2 * pair + 2].reshape(2 * block_cells, -1)
         first, second = [
             lax.dot_general(
@@ -82,21 +110,22 @@
             flat = jnp.where((query_col & bit) != 0, moved, flat)
         flat = flat * scale
         for a in range(window_side):
-            reply_ref[pair, a * window_side : (a + 1) * window_side, :] = flat[
+            base = (pair * window_side + a) * window_side
+            reply_ref[base : base + window_side, :] = flat[
                 a * span_side : a * span_side + window_side
             ]
 
 
 def assemble_kernel(pair_count, source_ref, half_ref, reply_ref, out_ref):
-    lanes = reply_ref.shape[2]
-    is_first = lax.broadcasted_iota(jnp.int32, reply_ref.shape[1:], 1) < lanes // 2
+    window_cells, lanes = out_ref.shape[1], reply_ref.shape[1]
+    is_first = lax.broadcasted_iota(jnp.int32, (window_cells, lanes), 1) < lanes // 2
     for level in range(LEVELS):
 
         def step(m, carry, level=level):
             at = 2 * (level * pair_count + m)
             picked = []
             for side in range(2):
-                rows = reply_ref[source_ref[at + side]]
+                rows = reply_ref[pl.ds(source_ref[at + side] * window_cells, window_cells), :]
                 moved = pltpu.roll(rows, lanes // 2, 1)
                 picked.append(jnp.where(half_ref[at + side] == side, rows, moved))
             spot = pl.ds(pl.multiple_of(m * lanes, lanes), lanes)
@@ -111,55 +140,59 @@
     window_side = 2 * RADIUS + 1
     block_cells = tile_side * tile_side
     frame_count, band_rows, band_cols, channels = fmap1.shape
-    device_count = lax.axis_size("rows") * lax.axis_size("cols")
+    row_count = lax.axis_size("rows")
+    col_count = lax.axis_size("cols")
+    device_count = row_count * col_count
     tiles_across = band_cols // tile_side
     per_frame = band_rows // tile_side * tiles_across
     block_count = frame_count * per_frame
     owner_slots = max(2, (2 * block_count + device_count - 1) // device_count)
-    owner_slots += owner_slots % 2
-    slot_count = LEVELS * owner_slots
+    row_slots = -(-owner_slots * col_count // STEP_SLOTS) * STEP_SLOTS
+    slot_count = LEVELS * row_slots
     pair_slots = slot_count // 2
     queries = fmap1.reshape(
         frame_count, band_rows // tile_side, tile_side, tiles_across, tile_side, channels
     )
     queries = queries.transpose(0, 1, 3, 2, 4, 5).reshape(block_count, block_cells, channels)
     owner_ids = target_owner[:, :, 0]
-    peer_ids = jnp.arange(device_count, dtype=jnp.int32)
-    owner_hits = (owner_ids[:, :, None] == peer_ids[None, None, :]).astype(jnp.int32)
+    owner_rows = owner_ids // col_count
+    peer_ids = jnp.arange(row_count, dtype=jnp.int32)
+    owner_hits = (owner_rows[:, :, None] == peer_ids[None, None, :]).astype(jnp.int32)
     slot_rank = jnp.sum(owner_hits * (jnp.cumsum(owner_hits, axis=1) - 1), axis=2)
     block_ids = jnp.arange(block_count, dtype=jnp.int32)
     label_rows = []
     for level in range(LEVELS):
         tile_count = (band_rows >> level) // tile_side * ((band_cols >> level) // tile_side)
-        label_rows.append(block_ids // per_frame * per_frame + target_tile[level] % tile_count)
-    rank_ids = jnp.arange(owner_slots, dtype=jnp.int32)
+        regions = block_ids // per_frame * col_count + owner_ids[level] % col_count
+        label_rows.append(regions * per_frame + target_tile[level] % tile_count)
+    rank_ids = jnp.arange(row_slots, dtype=jnp.int32)
     rank_hits = (slot_rank[:, :, None] == rank_ids[None, None, :]).astype(jnp.int32)
     slot_hits = owner_hits[:, :, :, None] * rank_hits[:, :, None, :]
 
     def by_slot(values):
         table = jnp.sum(slot_hits * values[:, :, None, None], axis=1)
-        return table.transpose(1, 0, 2).reshape(device_count, slot_count)
+        return table.transpose(1, 0, 2).reshape(row_count, slot_count)
 
     labels_sent = by_slot(jnp.stack(label_rows))
     blocks_sent = by_slot(jnp.broadcast_to(block_ids[None], owner_ids.shape))
     slot_block = (slot_count, block_cells, channels)
-    slot_total = device_count * slot_count
+    slot_total = row_count * slot_count
     queries_sent = pl.pallas_call(
         functools.partial(dispatch_kernel, slot_count),
         out_shape=jax.ShapeDtypeStruct((slot_total,) + slot_block[1:], jnp.bfloat16),
         grid_spec=pltpu.PrefetchScalarGridSpec(
             num_scalar_prefetch=1,
-            grid=(device_count,),
+            grid=(row_count,),
             in_specs=[pl.BlockSpec(queries.shape, lambda d, *_: (0, 0, 0))],
             out_specs=pl.BlockSpec(slot_block, lambda d, *_: (d, 0, 0)),
         ),
     )(blocks_sent.reshape(-1), queries)
     label_part = lax.all_to_all(
-        labels_sent, ("rows", "cols"), split_axis=0, concat_axis=0, tiled=True
+        labels_sent, "rows", split_axis=0, concat_axis=0, tiled=True
     )
     query_part = lax.all_to_all(
-        queries_sent.reshape((device_count,) + slot_block),
-        ("rows", "cols"),
+        queries_sent.reshape((row_count,) + slot_block),
+        "rows",
         split_axis=0,
         concat_axis=0,
         tiled=True,
@@ -170,37 +203,49 @@
     maps = []
     plan = []
     for level_map in levels:
-        padded = padded_2(level_map, (("rows", 1), ("cols", 2)), RADIUS).astype(jnp.float32)
+        across = level_map.shape[2] // tile_side
+        band = lax.all_gather(level_map, "cols", axis=2, tiled=True)
+        padded = padded_2(band, (("rows", 1),), RADIUS).astype(jnp.float32)
+        padded = jnp.pad(padded, ((0, 0), (0, 0), (RADIUS, RADIUS), (0, 0)))
         maps.append(padded.reshape((-1,) + padded.shape[2:]))
-        plan.append((padded.shape[1], level_map.shape[2] // tile_side))
+        plan.append((padded.shape[1], across))
     window_cells = window_side * window_side
-    reply_block = (pair_slots, window_cells, 2 * block_cells)
+    span_side = 4 * RADIUS
+    step_block = (STEP_SLOTS, block_cells, channels)
+    reply_block = (STEP_SLOTS // 2 * window_cells, 2 * block_cells)
     replies = pl.pallas_call(
         functools.partial(
-            correlate_kernel, (per_frame, tuple(plan)), channels ** (-0.5), slot_count
+            correlate_kernel,
+            (per_frame, col_count, tuple(plan)),
+            channels ** (-0.5),
+            slot_count,
         ),
         out_shape=jax.ShapeDtypeStruct(
-            (device_count * pair_slots,) + reply_block[1:], jnp.float32
+            (row_count * pair_slots * window_cells, 2 * block_cells), jnp.float32
         ),
         grid_spec=pltpu.PrefetchScalarGridSpec(
             num_scalar_prefetch=1,
-            grid=(device_count,),
-            in_specs=[pl.BlockSpec(slot_block, lambda d, *_: (d, 0, 0))]
-            + [pl.BlockSpec(level_map.shape, lambda d, *_: (0, 0, 0)) for level_map in maps],
-            out_specs=pl.BlockSpec(reply_block, lambda d, *_: (d, 0, 0)),
+            grid=(slot_total // STEP_SLOTS,),
+            in_specs=[pl.BlockSpec(step_block, lambda d, *_: (d, 0, 0))]
+            + [pl.BlockSpec(memory_space=pltpu.HBM)] * LEVELS,
+            out_specs=pl.BlockSpec(reply_block, lambda d, *_: (d, 0)),
+            scratch_shapes=[
+                pltpu.VMEM((2, STEP_SLOTS, span_side, span_side, channels), jnp.float32),
+                pltpu.SemaphoreType.DMA((2, STEP_SLOTS)),
+            ],
         ),
     )(label_part.reshape(-1), query_part.reshape((slot_total,) + slot_block[1:]), *maps)
     returned = lax.all_to_all(
-        replies.reshape((device_count,) + reply_block),
-        ("rows", "cols"),
+        replies.reshape(row_count, pair_slots * window_cells, 2 * block_cells),
+        "rows",
         split_axis=0,
         concat_axis=0,
         tiled=True,
     )
     level_ids = jnp.arange(LEVELS, dtype=jnp.int32)[:, None]
-    slot_ids = level_ids * owner_slots + slot_rank
-    source_ids = owner_ids * pair_slots + slot_ids // 2
-    reply_table = returned.reshape((device_count * pair_slots,) + reply_block[1:])
+    slot_ids = level_ids * row_slots + slot_rank
+    source_ids = owner_rows * pair_slots + slot_ids // 2
+    reply_table = returned.reshape(-1, 2 * block_cells)
     return pl.pallas_call(
         functools.partial(assemble_kernel, block_count // 2),
         out_shape=jax.ShapeDtypeStruct(

time: 408 us -> 416 us (1.020)
  Pallas kernels: 52.5 us -> 82.4 us
  waiting for transfers between devices: 257 us -> 229 us
  other arithmetic: 15.1 us -> 31.8 us
  between operations: 0.27 us -> 13.6 us
  starting transfers between devices: 51.3 us -> 40.1 us
  local copies, waits for them, and re-layouts: 28.8 us -> 19 us
    all_gather x0 -> x2, waiting for transfers between devices: none -> 168 us  [body(): band = lax.all_gather(level_map, 'cols', axis=2, tiled=True)]
    all_to_all x3, waiting for transfers between devices: 144 us -> 60.3 us  [the longest x1 60.3 us: body(): lax.all_to_all(replies.reshape(row_count, pair_slots * window_cells, 2 *...]
    ppermute x4 -> x2, waiting for transfers between devices: 60.4 us -> 0.01 us  [padded_2(): lax.ppermute(lax.slice_in_dim(block, 0, width, axis=dim), axis, backward)]
    ppermute x4 -> x2, waiting for transfers between devices: 52.8 us -> 0.01 us  [padded_2(): lax.ppermute(lax.slice_in_dim(block, block.shape[dim] - width, None, axis...]
    pallas_call x1, Pallas kernels: 28.3 us -> 65.5 us  [body(): pl.pallas_call(functools.partial(correlate_kernel, (per_frame, col_count,...]
    concatenate x1 -> x2, other arithmetic: 0.1 us -> 11.5 us  [padded_2(): block = jnp.concatenate([low, block, high], axis=dim)]
    reshape x0 -> x2, other arithmetic: none -> 11.1 us  [body(): maps.append(padded.reshape((-1,) + padded.shape[2:]))]
    ppermute x4 -> x2, starting transfers between devices: 15.5 us -> 6.6 us  [padded_2(): lax.ppermute(lax.slice_in_dim(block, block.shape[dim] - width, None, axis...]
  transfers between devices with their start and end apart: 11 -> 9, of which waited for: 5 -> 3; matrix products, arithmetic and copies ran while one was open for 5% -> 8% of each run, Pallas kernels for 3% -> 2%
where the time goes in v2:
time: 416 us
  waiting for transfers between devices  229 us (55%)
  Pallas kernels  82.4 us (20%)
  starting transfers between devices  40.1 us (10%)
  other arithmetic  31.8 us (8%)
  local copies, waits for them, and re-layouts  19 us (5%)
  between operations  13.6 us (3%)
    all_gather x2, waiting for transfers between devices, body(): band = lax.all_gather(level_map, 'cols', axis=2, tiled=True)  168 us
    pallas_call x1, Pallas kernels, body(): pl.pallas_call(functools.partial(correlate_kernel, (per_frame, col_count,...  65.5 us
    all_to_all x1, waiting for transfers between devices, body(): lax.all_to_all(replies.reshape(row_count, pair_slots * window_cells, 2 *...  60.3 us
    all_to_all x1, starting transfers between devices, body(): lax.all_to_all(replies.reshape(row_count, pair_slots * window_cells, 2 *...  20.8 us
    concatenate x2, other arithmetic, padded_2(): block = jnp.concatenate([low, block, high], axis=dim)  11.5 us
    reshape x2, other arithmetic, body(): maps.append(padded.reshape((-1,) + padded.shape[2:]))  11.1 us
    pallas_call x1, Pallas kernels, body(): pl.pallas_call(functools.partial(assemble_kernel, block_count // 2), out_...  10 us
  transfers between devices with their start and end apart: 9, of which 3 were waited for; matrix products, arithmetic and copies ran while one was open for 8% of the time, Pallas kernels for 2%

profile of v2, /device:TPU:0, one launch (start us, length us, event | category | flops | bytes accessed | tf_op | source)
XLA Modules:
  0.0 415.5 jit_solution(1587704542376488209)
XLA Ops:
  6.5 5.2 %reshape.239 = f32[2,16,2,32,2,256]{5,4,3,2,1,0:T(2,128)} reshape(bf16[2,32,64,256]{3,2,1,0:T(8,128)(2,1)} %param.5) | data formatting | bytes 6291456 | tf_op jit(solution)/shard_map/reshape | solution.py:30
  11.8 5.5 %reduce_sum.39 = f32[2,16,32,256]{3,2,1,0:T(8,128)S(1)} reduce(f32[2,16,2,32,2,256]{5,4,3,2,1,0:T(2,128)} %reshape.239, f32[]{:T(128)} %constant.110.clone.1), dimensions={2,4}, to_apply=%region_4.5 | reduce | flops 786432 | bytes 5242884 | tf_op jit(solution)/shard_map/reduce_sum | solution.py:33
  17.2 0.9 multiply_convert_fusion
  21.8 5.2 %all-to-all-start = ((s32[8,1,32]{2,1,0:T(1,128)}), s32[8,1,32]{2,1,0:T(1,128)S(1)}, u32[]{:S(2)}, u32[]{:S(2)}) async-start(s32[8,1,32]{2,1,0:T(1,128)} %bitcast.4), calls=%async_computation | async-start | bytes 8192 | tf_op jit(solution)/shard_map/all_to_all | solution.py:190
  27.7 1.6 copy.16
  29.3 7.0 %shard_map.46 = bf16[256,64,256]{2,1,0:T(8,128)(2,1)} custom-call(s32[256]{0:T(256)} %reshape_reshape.3.block_ref, bf16[64,64,256]{2,1,0:T(8,128)(2,1)} %bitcast.33), custom_call_target="tpu_custom_call" | custom-call | tf_op jit(solution)/shard_map/pallas_call | solution.py:180
  36.2 5.0 %all-to-all-start.1 = ((bf16[8,32,64,256]{3,2,1,0:T(8,128)(2,1)}), bf16[8,32,64,256]{3,2,1,0:T(8,128)(2,1)}, u32[]{:S(2)}, u32[]{:S(2)}) async-start(bf16[8,32,64,256]{3,2,1,0:T(8,128)(2,1)} %bitcast.29), calls=%async_computation.1 | async-start | bytes 16777216 | tf_op jit(solution)/shard_map/all_to_all | solution.py:193
  41.2 25.5 %all-gather.5.cloned.1.call-done = bf16[2,16,128,256]{3,2,1,0:T(8,128)(2,1)} async-done(((bf16[2,16,32,256]{3,2,1,0:T(8,128)(2,1)}), bf16[2,16,128,256]{3,2,1,0:T(8,128)(2,1)}) %all-gather.5.cloned.1.call-update) | async-done | bytes 2097168 | tf_op jit(solution)/shard_map/all_gather | solution.py:207
  66.7 2.4 fusion.26
  69.2 1.3 collective-permute-start.3
  70.5 3.1 collective-permute-start.2
  74.8 142.0 %all-gather.3.cloned.1.call-done = bf16[2,32,256,256]{3,2,1,0:T(8,128)(2,1)} async-done(((bf16[2,32,64,256]{3,2,1,0:T(8,128)(2,1)}), bf16[2,32,256,256]{3,2,1,0:T(8,128)(2,1)}) %all-gather.3.cloned.1.call-update) | async-done | bytes 8388624 | tf_op jit(solution)/shard_map/all_gather | solution.py:207
  216.8 1.7 fusion.25
  218.5 1.3 collective-permute-start.1
  219.8 3.5 collective-permute-start
  223.3 1.9 fusion.11
  225.3 3.6 bitcast_convert_fusion.1.refs_1_
  228.9 9.5 %fusion.5 = bf16[2,40,264,256]{3,2,1,0:T(8,128)(2,1)S(1)} fusion(bf16[2,4,256,256]{3,2,1,0:T(8,128)(2,1)S(1)} %collective-permute-done.1, bf16[2,32,256,256]{3,2,1,0:T(8,128)(2,1)S(1)} %bitcast.32, bf16[2,4,256,256]{3,2,1,0:T(8,128)(2,1)S(1)} %collective-permute-done), kind=kLoop, calls=%fused_computation.7 | loop fusion | flops 64880640 | bytes 21299200 | tf_op jit(solution)/shard_map/concatenate | solution.py:24
  238.4 7.5 %bitcast_convert_fusion.refs_0_ = f32[80,264,256]{2,1,0:T(8,128)} fusion(bf16[2,40,264,256]{3,2,1,0:T(8,128)(2,1)S(1)} %fusion.5), kind=kLoop, calls=%fused_computation.8 | loop fusion | flops 5406720 | bytes 32440320 | tf_op jit(solution)/shard_map/reshape | solution.py:210
  246.0 65.5 %shard_map.47 = f32[10368,128]{1,0:T(8,128)} custom-call(s32[256]{0:T(256)} %reshape.223.label_ref, bf16[256,64,256]{2,1,0:T(8,128)(2,1)} %bitcast.10.query_ref, f32[80,264,256]{2,1,0:T(8,128)} %bitcast_convert_fusion.refs_0_, f32[48,136,256]{2,1,0:T(8,128)} %bitcast_convert_fusion.1.refs_1_), custom_call_target="tpu_custom_call" | custom-call | tf_op jit(solution)/shard_map/pallas_call | solution.py:216
  311.4 20.8 %all-to-all-start.2 = ((f32[8,1296,128]{2,1,0:T(8,128)}), f32[8,1296,128]{2,1,0:T(8,128)}, u32[]{:S(2)}, u32[]{:S(2)}) async-start(f32[8,1296,128]{2,1,0:T(8,128)} %bitcast.30), calls=%async_computation.2 | async-start | bytes 10616832 | tf_op jit(solution)/shard_map/all_to_all | solution.py:238
  333.0 60.3 %all-to-all-done.2 = f32[8,1296,128]{2,1,0:T(8,128)} async-done(((f32[8,1296,128]{2,1,0:T(8,128)}), f32[8,1296,128]{2,1,0:T(8,128)}, u32[]{:S(2)}, u32[]{:S(2)}) %all-to-all-start.2) | async-done | bytes 5308448 | tf_op jit(solution)/shard_map/all_to_all | solution.py:238
  393.3 10.0 %shard_map.48 = f32[2,81,4096]{2,1,0:T(8,128)} custom-call(s32[128]{0:T(128)} %get-tuple-element.16.source_ref, s32[128]{0:T(128)} %get-tuple-element.15.half_ref, f32[10368,128]{1,0:T(8,128)} %bitcast.14.reply_ref), custom_call_target="tpu_custom_call" | custom-call | tf_op jit(solution)/shard_map/pallas_call | solution.py:249
  403.3 5.4 %copy.17 = f32[2,81,4096]{2,0,1:T(2,128)} copy(f32[2,81,4096]{2,1,0:T(8,128)} %shard_map.48) | data formatting | bytes 5308416 | tf_op jit(solution)/shard_map/pallas_call | solution.py:249
  (44 shorter events, 6.4 us)
Async XLA Ops:
  6.5 12.9 %copy-start.2 = (s32[2,64,1]{1,2,0:T(1,128)S(1)}, s32[2,64,1]{1,2,0:T(1,128)}, u32[]{:S(2)}) copy-start(s32[2,64,1]{1,2,0:T(1,128)} %param.6) | copy-start | bytes 1540
  6.5 13.8 %copy-start.3 = (s32[2,64]{1,0:T(2,128)S(1)}, s32[2,64]{1,0:T(2,128)}, u32[]{:S(2)}) copy-start(s32[2,64]{1,0:T(2,128)} %param.7) | copy-start | bytes 1540
  6.5 21.1 %copy-start.1 = (bf16[2,32,64,256]{3,2,1,0:T(8,128)(2,1)S(1)}, bf16[2,32,64,256]{3,2,1,0:T(8,128)(2,1)}, u32[]{:S(2)}) copy-start(bf16[2,32,64,256]{3,2,1,0:T(8,128)(2,1)} %param.4) | copy-start | bytes 6291460
  6.5 60.2 %all-gather.5.cloned.1.call-start = ((), (), s32[]{:S(2)}) async-start(), calls=%async_computation.4 | async-start | bytes 2621440 | tf_op jit(solution)/shard_map/all_gather | solution.py:207
  18.2 198.6 %all-gather.3.cloned.1.call-start = ((), (), s32[]{:S(2)}) async-start(), calls=%async_computation.3 | async-start | bytes 10485760 | tf_op jit(solution)/shard_map/all_gather | solution.py:207
  21.8 14.4 %all-to-all-start = ((s32[8,1,32]{2,1,0:T(1,128)}), s32[8,1,32]{2,1,0:T(1,128)S(1)}, u32[]{:S(2)}, u32[]{:S(2)}) async-start(s32[8,1,32]{2,1,0:T(1,128)} %bitcast.4), calls=%async_computation | async-start | bytes 8192 | tf_op jit(solution)/shard_map/all_to_all | solution.py:190
  36.2 209.7 %all-to-all-start.1 = ((bf16[8,32,64,256]{3,2,1,0:T(8,128)(2,1)}), bf16[8,32,64,256]{3,2,1,0:T(8,128)(2,1)}, u32[]{:S(2)}, u32[]{:S(2)}) async-start(bf16[8,32,64,256]{3,2,1,0:T(8,128)(2,1)} %bitcast.29), calls=%async_computation.1 | async-start | bytes 16777216 | tf_op jit(solution)/shard_map/all_to_all | solution.py:193
  66.7 156.6 %copy-start = (bf16[2,16,128,256]{3,2,1,0:T(8,128)(2,1)S(1)}, bf16[2,16,128,256]{3,2,1,0:T(8,128)(2,1)}, u32[]{:S(2)}) copy-start(bf16[2,16,128,256]{3,2,1,0:T(8,128)(2,1)} %all-gather.5.cloned.1.call-done) | copy-start | bytes 6291460
  69.2 154.1 %collective-permute-start.3 = (bf16[2,4,128,256]{3,2,1,0:T(8,128)(2,1)}, bf16[2,4,128,256]{3,2,1,0:T(8,128)(2,1)S(1)}, u32[]{:S(2)}, u32[]{:S(2)}) collective-permute-start(bf16[2,4,128,256]{3,2,1,0:T(8,128)(2,1)} %get-tuple-element.10), channel_id=1, source_target_pairs={{4,0},{8,4},{12,8},{16,12},{20,16},{24,20},{28,24},{5,1},{9,5},{13... | collective-permute-start | bytes 1572872 | tf_op jit(solution)/shard_map/ppermute | solution.py:23
  70.5 152.9 %collective-permute-start.2 = (bf16[2,4,128,256]{3,2,1,0:T(8,128)(2,1)}, bf16[2,4,128,256]{3,2,1,0:T(8,128)(2,1)S(1)}, u32[]{:S(2)}, u32[]{:S(2)}) collective-permute-start(bf16[2,4,128,256]{3,2,1,0:T(8,128)(2,1)} %get-tuple-element.9), channel_id=1, source_target_pairs={{0,4},{4,8},{8,12},{12,16},{16,20},{20,24},{24,28},{1,5},{5,9},{9,... | collective-permute-start | bytes 1572872 | tf_op jit(solution)/shard_map/ppermute | solution.py:20
  218.5 10.4 %collective-permute-start.1 = (bf16[2,4,256,256]{3,2,1,0:T(8,128)(2,1)S(1)}, bf16[2,4,256,256]{3,2,1,0:T(8,128)(2,1)S(1)}, u32[]{:S(2)}, u32[]{:S(2)}) collective-permute-start(bf16[2,4,256,256]{3,2,1,0:T(8,128)(2,1)S(1)} %get-tuple-element.8), channel_id=1, source_target_pairs={{4,0},{8,4},{12,8},{16,12},{20,16},{24,20},{28,24},{5,1},{9,5},{13... | collective-permute-start | bytes 3145736 | tf_op jit(solution)/shard_map/ppermute | solution.py:23
  219.8 9.1 %slice-start = ((s8[8388608]{0:T(1024)(128)(4,1)}), s8[4194304]{0:T(1024)(128)(4,1)S(1)}, s32[]{:S(2)}) async-start(s8[8388608]{0:T(1024)(128)(4,1)} %bitcast.31), calls=%async_computation.5 | async-start | bytes 8388608
  219.8 9.1 %collective-permute-start = (bf16[2,4,256,256]{3,2,1,0:T(8,128)(2,1)S(1)}, bf16[2,4,256,256]{3,2,1,0:T(8,128)(2,1)S(1)}, u32[]{:S(2)}, u32[]{:S(2)}) collective-permute-start(bf16[2,4,256,256]{3,2,1,0:T(8,128)(2,1)S(1)} %get-tuple-element.7), channel_id=1, source_target_pairs={{0,4},{4,8},{8,12},{12,16},{16,20},{20,24},{24,28},{1,5},{5,9},{9,... | collective-permute-start | bytes 3145736 | tf_op jit(solution)/shard_map/ppermute | solution.py:20
  225.3 3.6 slice-start.1
  311.4 81.9 %all-to-all-start.2 = ((f32[8,1296,128]{2,1,0:T(8,128)}), f32[8,1296,128]{2,1,0:T(8,128)}, u32[]{:S(2)}, u32[]{:S(2)}) async-start(f32[8,1296,128]{2,1,0:T(8,128)} %bitcast.30), calls=%async_computation.2 | async-start | bytes 10616832 | tf_op jit(solution)/shard_map/all_to_all | solution.py:238
Sparse Core Ops, SparseCore 0:
  18.3 48.3 all-gather.4
  68.3 148.4 all-gather.2

commit v3 on v1

v3 whole, which is shorter than its diff:
```python
import functools

import jax
import jax.numpy as jnp
from jax import lax
from jax.experimental import pallas as pl
from jax.experimental.pallas import tpu as pltpu
from jax.sharding import PartitionSpec as P

RADIUS = 4
LEVELS = 2
STEP_SLOTS = 16


def padded_2(block, sides, width):
    for axis, dim in sides:
        count = lax.axis_size(axis)
        forward = [(i, i + 1) for i in range(count - 1)]
        backward = [(target, source) for source, target in forward]
        low = lax.ppermute(
            lax.slice_in_dim(block, block.shape[dim] - width, None, axis=dim), axis, forward
        )
        high = lax.ppermute(lax.slice_in_dim(block, 0, width, axis=dim), axis, backward)
        block = jnp.concatenate([low, block, high], axis=dim)
    return block


def pool_level(level_map):
    frame_count, rows_in, cols_in, channels = level_map.shape
    pooled = level_map.astype(jnp.float32).reshape(
        frame_count, rows_in // 2, 2, cols_in // 2, 2, channels
    )
    return jnp.mean(pooled, axis=(2, 4)).astype(jnp.bfloat16)


def dispatch_kernel(slot_count, block_ref, query_ref, sent_ref):
    base = pl.program_id(0) * slot_count
    for slot in range(slot_count):
        sent_ref[slot] = query_ref[block_ref[base + slot]]


def correlate_kernel(plan, scale, label_ref, query_ref, map_ref, reply_ref):
    per_frame, col_count, padded_rows, across = plan
    tile_side = 2 * RADIUS
    span_side = 4 * RADIUS
    window_side = 2 * RADIUS + 1
    block_cells = tile_side * tile_side
    base = pl.program_id(0) * STEP_SLOTS
    lane = lax.broadcasted_iota(jnp.int32, (1, 1, 2 * block_cells), 2)
    query_row = lane % block_cells // tile_side
    query_col = lane[0] % tile_side
    is_first = lane[0] < block_cells

    def window(slot):
        label = label_ref[base + slot]
        tile = label % per_frame
        region = label // per_frame
        row = region // col_count * padded_rows + tile // across * tile_side
        col = (region % col_count * across + tile % across) * tile_side
        col = pl.multiple_of(col, tile_side)
        cells = map_ref[pl.ds(row, span_side), pl.ds(col, span_side), :]
        return cells.reshape(span_side * span_side, -1).astype(jnp.bfloat16)

    for pair in range(STEP_SLOTS // 2):
        queries = query_ref[2 * pair : 2 * pair + 2].reshape(2 * block_cells, -1)
        first, second = [
            lax.dot_general(
                window(2 * pair + half),
                queries,
                (((1,), (1,)), ((), ())),
                preferred_element_type=jnp.float32,
            )
            for half in range(2)
        ]
        scores = jnp.where(is_first, first, second)
        scores = scores.reshape(span_side, span_side, 2 * block_cells)
        for bit in (1, 2, 4):
            scores = jnp.where((query_row & bit) != 0, scores[bit:], scores[:-bit])
        flat = scores.reshape(window_side * span_side, 2 * block_cells)
        for bit in (1, 2, 4):
            moved = pltpu.roll(flat, flat.shape[0] - bit, 0)
            flat = jnp.where((query_col & bit) != 0, moved, flat)
        flat = flat * scale
        for a in range(window_side):
            at = (pair * window_side + a) * window_side
            reply_ref[at : at + window_side, :] = flat[
                a * span_side : a * span_side + window_side
            ]


def assemble_kernel(pair_count, source_ref, half_ref, *refs):
    reply_refs, out_ref = refs[:-1], refs[-1]
    window_cells, lanes = out_ref.shape[1], reply_refs[0].shape[1]
    is_first = lax.broadcasted_iota(jnp.int32, (window_cells, lanes), 1) < lanes // 2
    for level in range(LEVELS):

        def step(m, carry, level=level):
            at = 2 * (level * pair_count + m)
            picked = []
            for side in range(2):
                first_row = source_ref[at + side] * window_cells
                rows = reply_refs[level][pl.ds(first_row, window_cells), :]
                moved = pltpu.roll(rows, lanes // 2, 1)
                picked.append(jnp.where(half_ref[at + side] == side, rows, moved))
            spot = pl.ds(pl.multiple_of(m * lanes, lanes), lanes)
            out_ref[level, :, spot] = jnp.where(is_first, picked[0], picked[1])
            return carry

        lax.fori_loop(0, pair_count, step, 0)


def body(fmap1, fmap2, target_owner, target_tile):
    tile_side = 2 * RADIUS
    window_side = 2 * RADIUS + 1
    block_cells = tile_side * tile_side
    frame_count, band_rows, band_cols, channels = fmap1.shape
    row_count = lax.axis_size("rows")
    col_count = lax.axis_size("cols")
    device_count = row_count * col_count
    tiles_across = band_cols // tile_side
    per_frame = band_rows // tile_side * tiles_across
    block_count = frame_count * per_frame
    owner_slots = max(2, (2 * block_count + device_count - 1) // device_count)
    row_slots = -(-owner_slots * col_count // STEP_SLOTS) * STEP_SLOTS
    pair_slots = row_slots // 2
    queries = fmap1.reshape(
        frame_count, band_rows // tile_side, tile_side, tiles_across, tile_side, channels
    )
    queries = queries.transpose(0, 1, 3, 2, 4, 5).reshape(block_count, block_cells, channels)
    owner_ids = target_owner[:, :, 0]
    owner_rows = owner_ids // col_count
    peer_ids = jnp.arange(row_count, dtype=jnp.int32)
    owner_hits = (owner_rows[:, :, None] == peer_ids[None, None, :]).astype(jnp.int32)
    slot_rank = jnp.sum(owner_hits * (jnp.cumsum(owner_hits, axis=1) - 1), axis=2)
    block_ids = jnp.arange(block_count, dtype=jnp.int32)
    label_rows = []
    for level in range(LEVELS):
        tile_count = (band_rows >> level) // tile_side * ((band_cols >> level) // tile_side)
        regions = block_ids // per_frame * col_count + owner_ids[level] % col_count
        label_rows.append(regions * per_frame + target_tile[level] % tile_count)
    rank_ids = jnp.arange(row_slots, dtype=jnp.int32)
    rank_hits = (slot_rank[:, :, None] == rank_ids[None, None, :]).astype(jnp.int32)
    slot_hits = owner_hits[:, :, :, None] * rank_hits[:, :, None, :]

    def by_slot(values):
        table = jnp.sum(slot_hits * values[:, :, None, None], axis=1)
        return table.transpose(1, 0, 2)

    labels_sent = by_slot(jnp.stack(label_rows))
    blocks_sent = by_slot(jnp.broadcast_to(block_ids[None], owner_ids.shape))
    slot_block = (row_slots, block_cells, channels)
    slot_total = row_count * row_slots
    label_part = lax.all_to_all(labels_sent, "rows", split_axis=0, concat_axis=0, tiled=True)
    levels = [fmap2]
    for level in range(1, LEVELS):
        levels.append(pool_level(levels[-1]))
    window_cells = window_side * window_side
    step_block = (STEP_SLOTS, block_cells, channels)
    reply_block = (STEP_SLOTS // 2 * window_cells, 2 * block_cells)
    reply_tables = [None] * LEVELS
    earlier = None
    for level in reversed(range(LEVELS)):
        queries_sent = pl.pallas_call(
            functools.partial(dispatch_kernel, row_slots),
            out_shape=jax.ShapeDtypeStruct((slot_total,) + slot_block[1:], jnp.bfloat16),
            grid_spec=pltpu.PrefetchScalarGridSpec(
                num_scalar_prefetch=1,
                grid=(row_count,),
                in_specs=[pl.BlockSpec(queries.shape, lambda d, *_: (0, 0, 0))],
                out_specs=pl.BlockSpec(slot_block, lambda d, *_: (d, 0, 0)),
            ),
        )(blocks_sent[:, level].reshape(-1), queries)
        query_part = lax.all_to_all(
            queries_sent.reshape((row_count,) + slot_block),
            "rows",
            split_axis=0,
            concat_axis=0,
            tiled=True,
        )
        band = lax.all_gather(levels[level], "cols", axis=2, tiled=True)
        if earlier is not None:
            band = lax.optimization_barrier((band, earlier))[0]
        padded = padded_2(band, (("rows", 1),), RADIUS).astype(jnp.float32)
        padded = jnp.pad(padded, ((0, 0), (0, 0), (RADIUS, RADIUS), (0, 0)))
        level_map = padded.reshape((-1,) + padded.shape[2:])
        plan = (per_frame, col_count, padded.shape[1], levels[level].shape[2] // tile_side)
        replies = pl.pallas_call(
            functools.partial(correlate_kernel, plan, channels ** (-0.5)),
            out_shape=jax.ShapeDtypeStruct(
                (row_count * pair_slots * window_cells, 2 * block_cells), jnp.float32
            ),
            grid_spec=pltpu.PrefetchScalarGridSpec(
                num_scalar_prefetch=1,
                grid=(slot_total // STEP_SLOTS,),
                in_specs=[
                    pl.BlockSpec(step_block, lambda d, *_: (d, 0, 0)),
                    pl.BlockSpec(
                        level_map.shape, lambda d, *_: (0, 0, 0), pipeline_mode=pl.Buffered(1)
                    ),
                ],
                out_specs=pl.BlockSpec(reply_block, lambda d, *_: (d, 0)),
            ),
        )(
            label_part[:, level].reshape(-1),
            query_part.reshape((slot_total,) + slot_block[1:]),
            level_map,
        )
        returned = lax.all_to_all(
            replies.reshape(row_count, pair_slots * window_cells, 2 * block_cells),
            "rows",
            split_axis=0,
            concat_axis=0,
            tiled=True,
        )
        earlier = returned
        reply_tables[level] = returned.reshape(-1, 2 * block_cells)
    source_ids = owner_rows * pair_slots + slot_rank // 2
    return pl.pallas_call(
        functools.partial(assemble_kernel, block_count // 2),
        out_shape=jax.ShapeDtypeStruct(
            (LEVELS, window_cells, block_count * block_cells), jnp.float32
        ),
        in_specs=[
            pl.BlockSpec(memory_space=pltpu.SMEM),
            pl.BlockSpec(memory_space=pltpu.SMEM),
        ]
        + [pl.BlockSpec(memory_space=pltpu.VMEM)] * LEVELS,
        out_specs=pl.BlockSpec(memory_space=pltpu.VMEM),
    )(source_ids.reshape(-1), (slot_rank % 2).reshape(-1), *reply_tables)


def solution(mesh):
    in_specs = (
        P(None, "rows", "cols", None),
        P(None, "rows", "cols", None),
        P(None, ("rows", "cols"), None),
        P(None, ("rows", "cols")),
    )
    out_specs = P(None, None, ("rows", "cols"))
    return jax.shard_map(body, mesh=mesh, in_specs=in_specs, out_specs=out_specs, check_vma=False)
```

time: 408 us -> 368 us (0.902)
  waiting for transfers between devices: 257 us -> 165 us
  blocking collectives: 0 us -> 52 us
  starting transfers between devices: 51.3 us -> 32.3 us
  other arithmetic: 15.1 us -> 33.8 us
  between operations: 0.27 us -> 13.5 us
  local copies, waits for them, and re-layouts: 28.8 us -> 20.6 us
    all_gather x0 -> x2, waiting for transfers between devices: none -> 91.1 us  [body(): band = lax.all_gather(levels[level], 'cols', axis=2, tiled=True)]
    all_to_all x3 -> x4, waiting for transfers between devices: 144 us -> 70.2 us  [the longest x2 38.4 us: body(): lax.all_to_all(queries_sent.reshape((row_count,) + slot_block), 'rows', s...]
    ppermute x4 -> x2, waiting for transfers between devices: 60.4 us -> 3.19 us  [padded_2(): lax.ppermute(lax.slice_in_dim(block, 0, width, axis=dim), axis, backward)]
    ppermute x4 -> x2, waiting for transfers between devices: 52.8 us -> 0.01 us  [padded_2(): lax.ppermute(lax.slice_in_dim(block, block.shape[dim] - width, None, axis...]
    all_to_all x0 -> x1, blocking collectives: none -> 52 us  [body(): lax.all_to_all(replies.reshape(row_count, pair_slots * window_cells, 2 *...]
    concatenate x1 -> x2, other arithmetic: 0.1 us -> 14 us  [padded_2(): block = jnp.concatenate([low, block, high], axis=dim)]
    ppermute x4 -> x2, starting transfers between devices: 15.5 us -> 3.58 us  [padded_2(): lax.ppermute(lax.slice_in_dim(block, block.shape[dim] - width, None, axis...]
    reshape x0 -> x2, other arithmetic: none -> 11.1 us  [body(): level_map = padded.reshape((-1,) + padded.shape[2:])]
  transfers between devices with their start and end apart: 11 -> 10, of which waited for: 5 -> 6; matrix products, arithmetic and copies ran while one was open for 5% -> 9% of each run, Pallas kernels for 3% -> 6%
where the time goes in v3:
time: 368 us; the launch traced here: 367 us
  waiting for transfers between devices  165 us (45%)
  blocking collectives  52 us (14%)
  Pallas kernels  49.7 us (14%)
  other arithmetic  33.8 us (9%)
  starting transfers between devices  32.3 us (9%)
  local copies, waits for them, and re-layouts  20.6 us (6%)
  between operations  13.5 us (4%)
    all_gather x2, waiting for transfers between devices, body(): band = lax.all_gather(levels[level], 'cols', axis=2, tiled=True)  91.1 us
    all_to_all x1, blocking collectives, body(): lax.all_to_all(replies.reshape(row_count, pair_slots * window_cells, 2 *...  52 us
    all_to_all x2, waiting for transfers between devices, body(): lax.all_to_all(queries_sent.reshape((row_count,) + slot_block), 'rows', s...  38.4 us
    all_to_all x1, waiting for transfers between devices, body(): lax.all_to_all(replies.reshape(row_count, pair_slots * window_cells, 2 *...  31.8 us
    pallas_call x2, Pallas kernels, body(): pl.pallas_call(functools.partial(correlate_kernel, plan, channels ** (-0....  28 us
    concatenate x2, other arithmetic, padded_2(): block = jnp.concatenate([low, block, high], axis=dim)  14 us
    pallas_call x2, Pallas kernels, body(): pl.pallas_call(functools.partial(dispatch_kernel, row_slots), out_shape=j...  11.7 us
    reshape x2, other arithmetic, body(): level_map = padded.reshape((-1,) + padded.shape[2:])  11.1 us
  transfers between devices with their start and end apart: 10, of which 6 were waited for; matrix products, arithmetic and copies ran while one was open for 9% of the time, Pallas kernels for 6%

profile of v3, /device:TPU:0, one launch (start us, length us, event | category | flops | bytes accessed | tf_op | source)
XLA Modules:
  0.0 367.0 jit_solution(10772768359629400416)
XLA Ops:
  6.5 5.2 %reshape.236 = f32[2,16,2,32,2,256]{5,4,3,2,1,0:T(2,128)} reshape(bf16[2,32,64,256]{3,2,1,0:T(8,128)(2,1)} %param.5) | data formatting | bytes 6291456 | tf_op jit(solution)/shard_map/reshape | solution.py:30
  11.8 5.5 %reduce_sum.42 = f32[2,16,32,256]{3,2,1,0:T(8,128)S(1)} reduce(f32[2,16,2,32,2,256]{5,4,3,2,1,0:T(2,128)} %reshape.236, f32[]{:T(128)} %constant.107.clone.1), dimensions={2,4}, to_apply=%region_4.5 | reduce | flops 786432 | bytes 5242884 | tf_op jit(solution)/shard_map/reduce_sum | solution.py:33
  21.8 5.2 %all-to-all-start = ((s32[8,2,16]{2,1,0:T(2,128)}), s32[8,2,16]{2,1,0:T(2,128)S(1)}, u32[]{:S(2)}, u32[]{:S(2)}) async-start(s32[8,2,16]{2,1,0:T(2,128)} %copy.10), calls=%async_computation | async-start | bytes 16384 | tf_op jit(solution)/shard_map/all_to_all | solution.py:153
  29.3 5.8 %shard_map.47 = bf16[128,64,256]{2,1,0:T(8,128)(2,1)} custom-call(s32[128]{0:T(128)} %reshape_squeeze.15.block_ref, bf16[64,64,256]{2,1,0:T(8,128)(2,1)} %bitcast.36), custom_call_target="tpu_custom_call" | custom-call | tf_op jit(solution)/shard_map/pallas_call | solution.py:163
  35.1 4.6 %all-to-all-start.2 = ((bf16[8,16,64,256]{3,2,1,0:T(8,128)(2,1)}), bf16[8,16,64,256]{3,2,1,0:T(8,128)(2,1)}, u32[]{:S(2)}, u32[]{:S(2)}) async-start(bf16[8,16,64,256]{3,2,1,0:T(8,128)(2,1)} %bitcast.38), calls=%async_computation.2 | async-start | bytes 8388608 | tf_op jit(solution)/shard_map/all_to_all | solution.py:173
  39.7 27.0 %all-gather.5.cloned.1.call-done = bf16[2,16,128,256]{3,2,1,0:T(8,128)(2,1)} async-done(((bf16[2,16,32,256]{3,2,1,0:T(8,128)(2,1)}), bf16[2,16,128,256]{3,2,1,0:T(8,128)(2,1)}) %all-gather.5.cloned.1.call-update) | async-done | bytes 2097168 | tf_op jit(solution)/shard_map/all_gather | solution.py:180
  71.6 3.2 collective-permute-done.1
  74.8 3.1 fusion.11
  77.9 3.5 bitcast_convert_fusion.1.map_ref
  81.4 7.4 %all-to-all-done.2 = bf16[8,16,64,256]{3,2,1,0:T(8,128)(2,1)} async-done(((bf16[8,16,64,256]{3,2,1,0:T(8,128)(2,1)}), bf16[8,16,64,256]{3,2,1,0:T(8,128)(2,1)}, u32[]{:S(2)}, u32[]{:S(2)}) %all-to-all-start.2) | async-done | bytes 4194336 | tf_op jit(solution)/shard_map/all_to_all | solution.py:173
  88.8 11.9 %shard_map.48 = f32[5184,128]{1,0:T(8,128)} custom-call(s32[128]{0:T(128)} %reshape_squeeze.14.label_ref, bf16[128,64,256]{2,1,0:T(8,128)(2,1)} %bitcast.12.query_ref, f32[48,136,256]{2,1,0:T(8,128)} %bitcast_convert_fusion.1.map_ref), custom_call_target="tpu_custom_call" | custom-call | tf_op jit(solution)/shard_map/pallas_call | solution.py:187
  100.7 52.0 %all_to_all.25 = f32[8,648,128]{2,1,0:T(8,128)} all-to-all(f32[8,648,128]{2,1,0:T(8,128)} %bitcast.43), channel_id=1, replica_groups=mesh['rows'=8,'cols'=4] {'rows'}, dimensions={0} | all-to-all | bytes 5308416 | tf_op jit(solution)/shard_map/all_to_all | solution.py:208
  152.7 64.1 %all-gather.3.cloned.1.call-done = bf16[2,32,256,256]{3,2,1,0:T(8,128)(2,1)} async-done(((bf16[2,32,64,256]{3,2,1,0:T(8,128)(2,1)}), bf16[2,32,256,256]{3,2,1,0:T(8,128)(2,1)}) %all-gather.3.cloned.1.call-update) | async-done | bytes 8388624 | tf_op jit(solution)/shard_map/all_gather | solution.py:180
  218.4 2.0 collective-permute-start.2
  222.3 5.9 %shard_map.46 = bf16[128,64,256]{2,1,0:T(8,128)(2,1)} custom-call(s32[128]{0:T(128)} %reshape_squeeze.13.block_ref, bf16[64,64,256]{2,1,0:T(8,128)(2,1)} %bitcast.37), custom_call_target="tpu_custom_call" | custom-call | tf_op jit(solution)/shard_map/pallas_call | solution.py:163
  228.2 6.0 %all-to-all-start.1 = ((bf16[8,16,64,256]{3,2,1,0:T(8,128)(2,1)}), bf16[8,16,64,256]{3,2,1,0:T(8,128)(2,1)}, u32[]{:S(2)}, u32[]{:S(2)}) async-start(bf16[8,16,64,256]{3,2,1,0:T(8,128)(2,1)} %bitcast.39), calls=%async_computation.1 | async-start | bytes 8388608 | tf_op jit(solution)/shard_map/all_to_all | solution.py:173
  234.7 11.0 %fusion.5 = bf16[2,40,264,256]{3,2,1,0:T(8,128)(2,1)S(1)} fusion(bf16[2,4,256,256]{3,2,1,0:T(8,128)(2,1)} %collective-permute-done.3, bf16[2,32,256,256]{3,2,1,0:T(8,128)(2,1)} %all-gather.3.cloned.1.call-done, bf16[2,4,256,256]{3,2,1,0:T(8,128)(2,1)S(1)} %collective-permute-done.2), kind=kLoop, calls=%fused_computation.7 | loop fusion | flops 64880640 | bytes 21299200 | tf_op jit(solution)/shard_map/concatenate | solution.py:24
  245.7 7.5 %bitcast_convert_fusion.map_ref = f32[80,264,256]{2,1,0:T(8,128)} fusion(bf16[2,40,264,256]{3,2,1,0:T(8,128)(2,1)S(1)} %fusion.5), kind=kLoop, calls=%fused_computation.8 | loop fusion | flops 5406720 | bytes 32440320 | tf_op jit(solution)/shard_map/reshape | solution.py:185
  253.2 31.0 %all-to-all-done.1 = bf16[8,16,64,256]{3,2,1,0:T(8,128)(2,1)} async-done(((bf16[8,16,64,256]{3,2,1,0:T(8,128)(2,1)}), bf16[8,16,64,256]{3,2,1,0:T(8,128)(2,1)}, u32[]{:S(2)}, u32[]{:S(2)}) %all-to-all-start.1) | async-done | bytes 4194336 | tf_op jit(solution)/shard_map/all_to_all | solution.py:173
  284.2 16.1 %shard_map.49 = f32[5184,128]{1,0:T(8,128)} custom-call(s32[128]{0:T(128)} %reshape_squeeze.12.label_ref, bf16[128,64,256]{2,1,0:T(8,128)(2,1)} %bitcast.9.query_ref, f32[80,264,256]{2,1,0:T(8,128)} %bitcast_convert_fusion.map_ref), custom_call_target="tpu_custom_call" | custom-call | tf_op jit(solution)/shard_map/pallas_call | solution.py:187
  300.3 10.4 %all-to-all-start.4 = ((f32[8,648,128]{2,1,0:T(8,128)}), f32[8,648,128]{2,1,0:T(8,128)S(1)}, u32[]{:S(2)}, u32[]{:S(2)}) async-start(f32[8,648,128]{2,1,0:T(8,128)} %bitcast.40), calls=%async_computation.4 | async-start | bytes 5308416 | tf_op jit(solution)/shard_map/all_to_all | solution.py:208
  311.4 31.8 %all-to-all-done.4 = f32[8,648,128]{2,1,0:T(8,128)S(1)} async-done(((f32[8,648,128]{2,1,0:T(8,128)}), f32[8,648,128]{2,1,0:T(8,128)S(1)}, u32[]{:S(2)}, u32[]{:S(2)}) %all-to-all-start.4) | async-done | bytes 2654240 | tf_op jit(solution)/shard_map/all_to_all | solution.py:208
  344.8 10.1 %shard_map.50 = f32[2,81,4096]{2,1,0:T(8,128)} custom-call(s32[128]{0:T(128)} %get-tuple-element.22.source_ref, s32[128]{0:T(128)} %get-tuple-element.21.half_ref, f32[5184,128]{1,0:T(8,128)} %bitcast.42, f32[5184,128]{1,0:T(8,128)} %bitcast.41), custom_call_target="tpu_custom_call" | custom-call | tf_op jit(solution)/shard_map/pallas_call | solution.py:218
  354.8 5.4 %copy.12 = f32[2,81,4096]{2,0,1:T(2,128)} copy(f32[2,81,4096]{2,1,0:T(8,128)} %shard_map.50) | data formatting | bytes 5308416 | tf_op jit(solution)/shard_map/pallas_call | solution.py:218
  (43 shorter events, 18.1 us)
Async XLA Ops:
  6.5 12.9 %copy-start.2 = (s32[2,64,1]{1,2,0:T(1,128)S(1)}, s32[2,64,1]{1,2,0:T(1,128)}, u32[]{:S(2)}) copy-start(s32[2,64,1]{1,2,0:T(1,128)} %param.6) | copy-start | bytes 1540
  6.5 13.9 %copy-start.3 = (s32[2,64]{1,0:T(2,128)S(1)}, s32[2,64]{1,0:T(2,128)}, u32[]{:S(2)}) copy-start(s32[2,64]{1,0:T(2,128)} %param.7) | copy-start | bytes 1540
  6.5 21.2 %copy-start.1 = (bf16[2,32,64,256]{3,2,1,0:T(8,128)(2,1)S(1)}, bf16[2,32,64,256]{3,2,1,0:T(8,128)(2,1)}, u32[]{:S(2)}) copy-start(bf16[2,32,64,256]{3,2,1,0:T(8,128)(2,1)} %param.4) | copy-start | bytes 6291460
  6.5 60.2 %all-gather.5.cloned.1.call-start = ((), (), s32[]{:S(2)}) async-start(), calls=%async_computation.6 | async-start | bytes 2621440 | tf_op jit(solution)/shard_map/all_gather | solution.py:180
  18.2 198.6 %all-gather.3.cloned.1.call-start = ((), (), s32[]{:S(2)}) async-start(), calls=%async_computation.5 | async-start | bytes 10485760 | tf_op jit(solution)/shard_map/all_gather | solution.py:180
  21.8 13.3 %all-to-all-start = ((s32[8,2,16]{2,1,0:T(2,128)}), s32[8,2,16]{2,1,0:T(2,128)S(1)}, u32[]{:S(2)}, u32[]{:S(2)}) async-start(s32[8,2,16]{2,1,0:T(2,128)} %copy.10), calls=%async_computation | async-start | bytes 16384 | tf_op jit(solution)/shard_map/all_to_all | solution.py:153
  35.1 53.7 %all-to-all-start.2 = ((bf16[8,16,64,256]{3,2,1,0:T(8,128)(2,1)}), bf16[8,16,64,256]{3,2,1,0:T(8,128)(2,1)}, u32[]{:S(2)}, u32[]{:S(2)}) async-start(bf16[8,16,64,256]{3,2,1,0:T(8,128)(2,1)} %bitcast.38), calls=%async_computation.2 | async-start | bytes 8388608 | tf_op jit(solution)/shard_map/all_to_all | solution.py:173
  68.0 3.6 collective-permute-start
  69.6 5.2 %collective-permute-start.1 = (bf16[2,4,128,256]{3,2,1,0:T(8,128)(2,1)S(1)}, bf16[2,4,128,256]{3,2,1,0:T(8,128)(2,1)S(1)}, u32[]{:S(2)}, u32[]{:S(2)}) collective-permute-start(bf16[2,4,128,256]{3,2,1,0:T(8,128)(2,1)S(1)} %get-tuple-element.14), channel_id=1, source_target_pairs={{4,0},{8,4},{12,8},{16,12},{20,16},{24,20},{28,24},{5,1},{9,5},{13... | collective-permute-start | bytes 1572872 | tf_op jit(solution)/shard_map/ppermute | solution.py:23
  218.4 16.3 %collective-permute-start.2 = (bf16[2,4,256,256]{3,2,1,0:T(8,128)(2,1)S(1)}, bf16[2,4,256,256]{3,2,1,0:T(8,128)(2,1)S(1)}, u32[]{:S(2)}, u32[]{:S(2)}) collective-permute-start(bf16[2,4,256,256]{3,2,1,0:T(8,128)(2,1)S(1)} %get-tuple-element.11), channel_id=1, source_target_pairs={{0,4},{4,8},{8,12},{12,16},{16,20},{20,24},{24,28},{1,5},{5,9},{9,... | collective-permute-start | bytes 3145736 | tf_op jit(solution)/shard_map/ppermute | solution.py:20
  220.4 14.3 %collective-permute-start.3 = (bf16[2,4,256,256]{3,2,1,0:T(8,128)(2,1)S(1)}, bf16[2,4,256,256]{3,2,1,0:T(8,128)(2,1)}, u32[]{:S(2)}, u32[]{:S(2)}) collective-permute-start(bf16[2,4,256,256]{3,2,1,0:T(8,128)(2,1)S(1)} %get-tuple-element.12), channel_id=1, source_target_pairs={{4,0},{8,4},{12,8},{16,12},{20,16},{24,20},{28,24},{5,1},{9,5},{13... | collective-permute-start | bytes 3145736 | tf_op jit(solution)/shard_map/ppermute | solution.py:23
  228.2 56.1 %all-to-all-start.1 = ((bf16[8,16,64,256]{3,2,1,0:T(8,128)(2,1)}), bf16[8,16,64,256]{3,2,1,0:T(8,128)(2,1)}, u32[]{:S(2)}, u32[]{:S(2)}) async-start(bf16[8,16,64,256]{3,2,1,0:T(8,128)(2,1)} %bitcast.39), calls=%async_computation.1 | async-start | bytes 8388608 | tf_op jit(solution)/shard_map/all_to_all | solution.py:173
  300.3 42.9 %all-to-all-start.4 = ((f32[8,648,128]{2,1,0:T(8,128)}), f32[8,648,128]{2,1,0:T(8,128)S(1)}, u32[]{:S(2)}, u32[]{:S(2)}) async-start(f32[8,648,128]{2,1,0:T(8,128)} %bitcast.40), calls=%async_computation.4 | async-start | bytes 5308416 | tf_op jit(solution)/shard_map/all_to_all | solution.py:208
  343.3 1.5 copy-start
Sparse Core Ops, SparseCore 0:
  18.3 48.3 all-gather.4
  68.3 148.4 all-gather.2
